TPU v7x, 512 devices: a whole 4x8x8 slice. The times are simulated.
512 devices in a mesh: batch: 8 (over y_lo, x), rows: 8 (over z), chan: 8 (over y_hi, core).
Axes of the slice: x: 4, y: 8 (y_hi: 4, y_lo: 2; y = y_hi * 2 + y_lo), z: 8, core: 2. Of those that a mesh axis runs over, the one named last changes fastest.
Arguments:
- images: float32 [64, 24, 64, 32], P('batch', None, ('rows', 'chan')), may hold values from -6 to 6
- shift_mid: float32 [3, 24], replicated, may hold values from -1.75 to 1.75
- gain_mid: float32 [3, 24], replicated, may hold values from -0.3 to 0.3
- lower_mid: float32 [3, 24, 24], replicated, may hold values from -1.25 to 1.25
- upper_mid: float32 [3, 24, 24], replicated, may hold values from -1.25 to 1.25
- diag_mid: float32 [3, 24], replicated, may hold values from -0.3 to 0.3
- first_mid: bfloat16 [3, 9, 12, 512], replicated, may hold values from -0.625 to 0.625
- first_bias_mid: bfloat16 [3, 512], replicated, may hold values from -3 to 3
- second_mid: bfloat16 [3, 512, 512], replicated, may hold values from -0.25 to 0.25
- second_bias_mid: float32 [3, 512], replicated, may hold values from -3 to 3
- third_mid: bfloat16 [3, 9, 512, 24], replicated, may hold values from -0.09375 to 0.09375
- third_bias_mid: float32 [3, 24], replicated, may hold values from -3 to 3
- shift_top: float32 [2, 48], replicated, may hold values from -1.75 to 1.75
- gain_top: float32 [2, 48], replicated, may hold values from -0.3 to 0.3
- lower_top: float32 [2, 48, 48], replicated, may hold values from -0.875 to 0.875
- upper_top: float32 [2, 48, 48], replicated, may hold values from -0.875 to 0.875
- diag_top: float32 [2, 48], replicated, may hold values from -0.3 to 0.3
- first_top: bfloat16 [2, 9, 24, 512], replicated, may hold values from -0.4375 to 0.4375
- first_bias_top: bfloat16 [2, 512], replicated, may hold values from -3 to 3
- second_top: bfloat16 [2, 512, 512], replicated, may hold values from -0.25 to 0.25
- second_bias_top: float32 [2, 512], replicated, may hold values from -3 to 3
- third_top: bfloat16 [2, 9, 512, 48], replicated, may hold values from -0.09375 to 0.09375
- third_bias_top: float32 [2, 48], replicated, may hold values from -3 to 3
Outputs:
- latent_mid: float32 [64, 12, 64, 32], P('batch', None, ('rows', 'chan'))
- latent_top: float32 [64, 48, 32, 16], P(('batch', 'chan'), None, 'rows')
- loglik: float32 [64], P(('batch', 'chan'))
All inputs are finite; a program needn't handle non-finite values.
Results may differ from a plain program's by a relative error of at most 0.008.
Values may be sent and summed in bfloat16 or wider, within the bound.
A program may use at most 64 MiB of HBM per device.

v0:
```python
import math

import jax
import jax.numpy as jnp
from jax import lax
from jax.sharding import PartitionSpec as P

log_two_pi = math.log(2.0 * math.pi)


def padded_2(x, sides, width):
    edges = {}
    for axis, dim in sides:
        size, length = (lax.axis_size(axis), x.shape[dim])
        up = [(i, (i + 1) % size) for i in range(size - 1)]
        last = lax.slice_in_dim(x, length - width, length, axis=dim)
        first = lax.slice_in_dim(x, 0, width, axis=dim)
        edges[dim] = (
            lax.ppermute(last, axis, up),
            lax.ppermute(first, axis, [(b, a) for a, b in up]),
        )
    done = []
    for _, dim in sides:
        low, high = edges[dim]
        around = [(width, width) if d in done else (0, 0) for d in range(x.ndim)]
        x = jnp.concatenate([jnp.pad(low, around), x, jnp.pad(high, around)], axis=dim)
        done.append(dim)
    return x


def with_halo(block, sides, width):
    for axis, dim in sides:
        count = lax.axis_size(axis)
        forward = [(i, i + 1) for i in range(count - 1)]
        backward = [(target, source) for source, target in forward]
        low = lax.ppermute(
            lax.slice_in_dim(block, block.shape[dim] - width, None, axis=dim), axis, forward
        )
        high = lax.ppermute(lax.slice_in_dim(block, 0, width, axis=dim), axis, backward)
        block = jnp.concatenate([low, block, high], axis=dim)
    return block


def in_blocks(x, dim, length):
    lengths = x.shape
    pieces = x.reshape(*lengths[:dim], length, lengths[dim] // length, *lengths[dim + 1 :])
    return jnp.moveaxis(pieces, dim, 0)


def summed_on_arrival(x, axis, dim):
    length = lax.axis_size(axis)
    pieces = lax.all_to_all(in_blocks(x, dim, length), axis, 0, 0, tiled=True)
    return jnp.sum(pieces, axis=0)


def sent_to_all(x, axis):
    copies = jnp.broadcast_to(x, (lax.axis_size(axis), *x.shape))
    return lax.all_to_all(copies, axis, split_axis=0, concat_axis=0, tiled=True)


def over_copies(x, axis):
    everything = sent_to_all(x, axis)
    return jnp.sum(everything, axis=0)


def conv_in(rimmed, weights, rows_out):
    columns = rimmed.shape[3]
    padded = jnp.pad(rimmed, ((0, 0), (0, 0), (0, 0), (1, 1)))
    summed = None
    for tap_idx in range(9):
        row_off = tap_idx // 3
        col_off = tap_idx % 3
        window = padded[:, :, row_off : row_off + rows_out, col_off : col_off + columns]
        contrib = jnp.einsum(
            "bchw,co->bhwo", window, weights[tap_idx], preferred_element_type=jnp.float32
        )
        summed = contrib if summed is None else summed + contrib
    return summed


def conv_out(rimmed, weights):
    rows_out = rimmed.shape[1] - 2
    columns = rimmed.shape[2]
    padded = jnp.pad(rimmed, ((0, 0), (0, 0), (1, 1), (0, 0)))
    summed = None
    for tap_idx in range(9):
        row_off = tap_idx // 3
        col_off = tap_idx % 3
        window = padded[:, row_off : row_off + rows_out, col_off : col_off + columns, :]
        contrib = jnp.einsum(
            "bhwc,co->bohw", window, weights[tap_idx], preferred_element_type=jnp.float32
        )
        summed = contrib if summed is None else summed + contrib
    return summed


def hidden_layers(widened, first_w, first_b, second_w, second_b, rows_out):
    inner = conv_in(widened, first_w, rows_out) + first_b.astype(jnp.float32)[None, None, None, :]
    inner = jax.nn.relu(inner).astype(jnp.bfloat16)
    middle = jnp.einsum("bhwc,co->bhwo", inner, second_w, preferred_element_type=jnp.float32)
    return jax.nn.relu(middle + second_b[None, None, None, :])


def mid_hidden(coupled, first_w, first_b, second_w, second_b):
    rimmed = padded_2(coupled, ((("rows", "chan"), 2),), 1)
    middle = hidden_layers(rimmed, first_w, first_b, second_w, second_b, coupled.shape[2]).astype(
        jnp.bfloat16
    )
    return padded_2(middle, ((("rows", "chan"), 1),), 1)


def top_hidden(coupled, first_w, first_b, second_w, second_b):
    rimmed = with_halo(coupled, (("rows", 2),), 1)
    middle = hidden_layers(rimmed, first_w, first_b, second_w, second_b, coupled.shape[2]).astype(
        jnp.bfloat16
    )
    return with_halo(middle, (("rows", 1),), 1)


def flow_step(flow_state, params, hidden_fn):
    (
        shift_vec,
        gain_vec,
        lower_raw,
        upper_raw,
        diag_log,
        first_w,
        first_b,
        second_w,
        second_b,
        third_w,
        third_b,
    ) = params
    channels = flow_state.shape[1]
    half_chan = channels // 2
    cell_count = flow_state.shape[2] * flow_state.shape[3]
    mixed_state = (flow_state + shift_vec[None, :, None, None]) * jnp.exp(gain_vec)[
        None, :, None, None
    ]
    lower_mat = jnp.tril(lower_raw, -1) + jnp.eye(channels, dtype=jnp.float32)
    upper_mat = jnp.triu(upper_raw, 1) + jnp.diag(jnp.exp(diag_log))
    matrix = jnp.dot(lower_mat, upper_mat, precision=lax.Precision.HIGHEST)
    mixed_state = jnp.einsum("oc,bchw->bohw", matrix, mixed_state, precision=lax.Precision.HIGHEST)
    part_a = mixed_state[:, :half_chan]
    part_b = mixed_state[:, half_chan:]
    coupled = part_a.astype(jnp.bfloat16)
    rim_middle = hidden_fn(coupled, first_w, first_b, second_w, second_b)
    output = conv_out(rim_middle, third_w) + third_b[None, :, None, None]
    gate_pre = output[:, :half_chan] + 2.0
    updated = (part_b + output[:, half_chan:]) * jax.nn.sigmoid(gate_pre)
    step_term = cell_count * (jnp.sum(gain_vec) + jnp.sum(diag_log)) + jnp.sum(
        jax.nn.log_sigmoid(gate_pre), axis=(1, 2, 3)
    )
    return (jnp.concatenate([part_a, updated], axis=1), step_term)


def scale_pass(flow_state, params, hidden_fn):
    logdet = jnp.zeros((flow_state.shape[0],), jnp.float32)
    for step_num in range(params[0].shape[0]):
        flow_state, step_term = flow_step(
            flow_state, tuple((p[step_num] for p in params)), hidden_fn
        )
        logdet = logdet + step_term
    return (flow_state, logdet)


def gauss_terms(latent):
    return -0.5 * jnp.sum(latent * latent, axis=(1, 2, 3)) - 0.5 * log_two_pi * latent[0].size


def body(
    images,
    shift_mid,
    gain_mid,
    lower_mid,
    upper_mid,
    diag_mid,
    first_mid,
    first_bias_mid,
    second_mid,
    second_bias_mid,
    third_mid,
    third_bias_mid,
    shift_top,
    gain_top,
    lower_top,
    upper_top,
    diag_top,
    first_top,
    first_bias_top,
    second_top,
    second_bias_top,
    third_top,
    third_bias_top,
):
    params_mid = (
        shift_mid,
        gain_mid,
        lower_mid,
        upper_mid,
        diag_mid,
        first_mid,
        first_bias_mid,
        second_mid,
        second_bias_mid,
        third_mid,
        third_bias_mid,
    )
    params_top = (
        shift_top,
        gain_top,
        lower_top,
        upper_top,
        diag_top,
        first_top,
        first_bias_top,
        second_top,
        second_bias_top,
        third_top,
        third_bias_top,
    )
    images_dev, channels, height, columns = images.shape
    flow_state, logdet_mid = scale_pass(images, params_mid, mid_hidden)
    half_chan = channels // 2
    latent_mid = flow_state[:, :half_chan]
    kept_chan = flow_state[:, half_chan:]
    mid_part = gauss_terms(latent_mid) + logdet_mid
    grouped = lax.all_to_all(kept_chan, "chan", split_axis=0, concat_axis=2, tiled=True)
    group_imgs, group_chan, group_rows, group_cols = grouped.shape
    squeezed = grouped.reshape(
        group_imgs, group_chan, group_rows // 2, 2, group_cols // 2, 2
    ).transpose(0, 1, 3, 5, 2, 4)
    squeezed = squeezed.reshape(group_imgs, group_chan * 4, group_rows // 2, group_cols // 2)
    latent_top, logdet_top = scale_pass(squeezed, params_top, top_hidden)
    top_part = gauss_terms(latent_top) + logdet_top
    mid_own = summed_on_arrival(mid_part, "chan", 0)
    summed = over_copies(mid_own + top_part, "rows")
    total_dims = channels * height * lax.axis_size("rows") * lax.axis_size("chan") * columns
    return (latent_mid, latent_top, summed / total_dims)


def solution(mesh):
    placed = (
        P("batch", None, ("rows", "chan"), None),
        P(),
        P(),
        P(),
        P(),
        P(),
        P(),
        P(),
        P(),
        P(),
        P(),
        P(),
        P(),
        P(),
        P(),
        P(),
        P(),
        P(),
        P(),
        P(),
        P(),
        P(),
        P(),
    )
    return jax.shard_map(
        body,
        mesh=mesh,
        in_specs=placed,
        out_specs=(
            P("batch", None, ("rows", "chan"), None),
            P(("batch", "chan"), None, "rows", None),
            P(("batch", "chan")),
        ),
        check_vma=False,
    )
```

profile of v0, /device:TPU:6, one launch (start us, length us, event | category | flops | bytes accessed | tf_op | source)
XLA Modules:
  0.0 222.8 jit_solution(14348905123432826290)
XLA Ops:
  1.5 1.5 slice_reduce_fusion.8
  5.2 1.7 collective-permute-start
  6.9 1.3 collective-permute-start.1
  9.9 2.5 %collective-permute-done.1 = bf16[8,12,1,32]{3,1,0,2:T(8,128)(2,1)S(1)} collective-permute-done((bf16[8,12,1,32]{3,1,0,2:T(8,128)(2,1)S(1)}, bf16[8,12,1,32]{3,1,0,2:T(8,128)(2,1)S(1)}, u32[]{:S(2)}, u32[]{:S(2)}) %collective-permute-start.1) | collective-permute-done | bytes 6176 | tf_op jit(solution)/shard_map/ppermute | solution.py:20
  17.3 5.4 %collective-permute-start.2 = (bf16[8,1,32,512]{3,2,0,1:T(8,128)(2,1)S(1)}, bf16[8,1,32,512]{3,2,0,1:T(8,128)(2,1)S(1)}, u32[]{:S(2)}, u32[]{:S(2)}) collective-permute-start(bf16[8,1,32,512]{3,2,0,1:T(8,128)(2,1)S(1)} %bitcast.923), channel_id=1, source_target_pairs={{0,1},{1,2},{2,3},{3,4},{4,5},{5,6},{6,7},{7,8},{8,9},{9,10},{10,1... | collective-permute-start | bytes 786440 | tf_op jit(solution)/shard_map/ppermute | solution.py:19
  36.4 12.6 %collective-permute-start.4 = (bf16[8,12,1,32]{3,1,0,2:T(8,128)(2,1)S(1)}, bf16[8,12,1,32]{3,1,0,2:T(8,128)(2,1)S(1)}, u32[]{:S(2)}, u32[]{:S(2)}) collective-permute-start(bf16[8,12,1,32]{3,1,0,2:T(8,128)(2,1)S(1)} %slice.1912), channel_id=1, source_target_pairs={{0,1},{1,2},{2,3},{3,4},{4,5},{5,6},{6,7},{7,8},{8,9},{9,10},{10,1... | collective-permute-start | bytes 18440 | tf_op jit(solution)/shard_map/ppermute | solution.py:19
  50.3 1.8 collective-permute-done.5
  55.0 6.2 %collective-permute-start.6 = (bf16[8,1,32,512]{3,2,0,1:T(8,128)(2,1)S(1)}, bf16[8,1,32,512]{3,2,0,1:T(8,128)(2,1)S(1)}, u32[]{:S(2)}, u32[]{:S(2)}) collective-permute-start(bf16[8,1,32,512]{3,2,0,1:T(8,128)(2,1)S(1)} %bitcast.926), channel_id=1, source_target_pairs={{0,1},{1,2},{2,3},{3,4},{4,5},{5,6},{6,7},{7,8},{8,9},{9,10},{10,1... | collective-permute-start | bytes 786440 | tf_op jit(solution)/shard_map/ppermute | solution.py:19
  74.9 8.4 %collective-permute-start.8 = (bf16[8,12,1,32]{3,1,0,2:T(8,128)(2,1)S(1)}, bf16[8,12,1,32]{3,1,0,2:T(8,128)(2,1)S(1)}, u32[]{:S(2)}, u32[]{:S(2)}) collective-permute-start(bf16[8,12,1,32]{3,1,0,2:T(8,128)(2,1)S(1)} %slice.1916), channel_id=1, source_target_pairs={{0,1},{1,2},{2,3},{3,4},{4,5},{5,6},{6,7},{7,8},{8,9},{9,10},{10,1... | collective-permute-start | bytes 18440 | tf_op jit(solution)/shard_map/ppermute | solution.py:19
  89.3 6.5 %collective-permute-start.10 = (bf16[8,1,32,512]{3,2,0,1:T(8,128)(2,1)S(1)}, bf16[8,1,32,512]{3,2,0,1:T(8,128)(2,1)S(1)}, u32[]{:S(2)}, u32[]{:S(2)}) collective-permute-start(bf16[8,1,32,512]{3,2,0,1:T(8,128)(2,1)S(1)} %bitcast.929), channel_id=1, source_target_pairs={{0,1},{1,2},{2,3},{3,4},{4,5},{5,6},{6,7},{7,8},{8,9},{9,10},{10,1... | collective-permute-start | bytes 786440 | tf_op jit(solution)/shard_map/ppermute | solution.py:19
  97.1 2.1 collective-permute-done.11
  111.0 15.3 %all-to-all-start = ((f32[8,1,384]{2,1,0:T(1,128)}), f32[8,1,384]{2,1,0:T(1,128)S(1)}, u32[]{:S(2)}, u32[]{:S(2)}) async-start(f32[8,1,384]{2,1,0:T(1,128)} %reshape.1494), calls=%async_computation | async-start | bytes 24576 | tf_op jit(solution)/shard_map/all_to_all | solution.py:228
  126.5 7.5 %all-to-all-done = f32[8,1,384]{2,1,0:T(1,128)S(1)} async-done(((f32[8,1,384]{2,1,0:T(1,128)}), f32[8,1,384]{2,1,0:T(1,128)S(1)}, u32[]{:S(2)}, u32[]{:S(2)}) %all-to-all-start) | async-done | bytes 12320 | tf_op jit(solution)/shard_map/all_to_all | solution.py:228
  135.5 4.3 %collective-permute-start.12 = (bf16[1,24,1,16]{1,3,2,0:T(8,128)(2,1)S(1)}, bf16[1,24,1,16]{1,3,2,0:T(8,128)(2,1)S(1)}, u32[]{:S(2)}, u32[]{:S(2)}) collective-permute-start(bf16[1,24,1,16]{1,3,2,0:T(8,128)(2,1)S(1)} %get-tuple-element.52), channel_id=1, source_target_pairs={{0,8},{8,16},{16,24},{24,32},{32,40},{40,48},{48,56},{1,9},{9,17},... | collective-permute-start | bytes 2312 | tf_op jit(solution)/shard_map/ppermute | solution.py:36
  141.1 4.5 %collective-permute-done.13 = bf16[1,24,1,16]{1,3,2,0:T(8,128)(2,1)S(1)} collective-permute-done((bf16[1,24,1,16]{1,3,2,0:T(8,128)(2,1)S(1)}, bf16[1,24,1,16]{1,3,2,0:T(8,128)(2,1)S(1)}, u32[]{:S(2)}, u32[]{:S(2)}) %collective-permute-start.13) | collective-permute-done | bytes 800 | tf_op jit(solution)/shard_map/ppermute | solution.py:39
  147.2 14.0 %collective-permute-start.14 = (bf16[1,1,16,512]{3,2,1,0:T(8,128)(2,1)S(1)}, bf16[1,1,16,512]{3,2,1,0:T(8,128)(2,1)S(1)}, u32[]{:S(2)}, u32[]{:S(2)}) collective-permute-start(bf16[1,1,16,512]{3,2,1,0:T(8,128)(2,1)S(1)} %get-tuple-element.42), channel_id=1, source_target_pairs={{0,8},{8,16},{16,24},{24,32},{32,40},{40,48},{48,56},{1,9},{9,17},... | collective-permute-start | bytes 49160 | tf_op jit(solution)/shard_map/ppermute | solution.py:36
  164.0 2.8 %collective-permute-done.15 = bf16[1,1,16,512]{3,2,1,0:T(8,128)(2,1)S(1)} collective-permute-done((bf16[1,1,16,512]{3,2,1,0:T(8,128)(2,1)S(1)}, bf16[1,1,16,512]{3,2,1,0:T(8,128)(2,1)S(1)}, u32[]{:S(2)}, u32[]{:S(2)}) %collective-permute-start.15) | collective-permute-done | bytes 16416 | tf_op jit(solution)/shard_map/ppermute | solution.py:39
  169.2 3.9 %collective-permute-start.16 = (bf16[1,24,1,16]{1,3,2,0:T(8,128)(2,1)S(1)}, bf16[1,24,1,16]{1,3,2,0:T(8,128)(2,1)S(1)}, u32[]{:S(2)}, u32[]{:S(2)}) collective-permute-start(bf16[1,24,1,16]{1,3,2,0:T(8,128)(2,1)S(1)} %get-tuple-element.50), channel_id=1, source_target_pairs={{0,8},{8,16},{16,24},{24,32},{32,40},{40,48},{48,56},{1,9},{9,17},... | collective-permute-start | bytes 2312 | tf_op jit(solution)/shard_map/ppermute | solution.py:36
  181.0 4.5 %collective-permute-start.18 = (bf16[1,1,16,512]{3,2,1,0:T(8,128)(2,1)S(1)}, bf16[1,1,16,512]{3,2,1,0:T(8,128)(2,1)S(1)}, u32[]{:S(2)}, u32[]{:S(2)}) collective-permute-start(bf16[1,1,16,512]{3,2,1,0:T(8,128)(2,1)S(1)} %get-tuple-element.40), channel_id=1, source_target_pairs={{0,8},{8,16},{16,24},{24,32},{32,40},{40,48},{48,56},{1,9},{9,17},... | collective-permute-start | bytes 49160 | tf_op jit(solution)/shard_map/ppermute | solution.py:36
  187.5 3.3 %all-to-all-start.1 = ((f32[8,1,1]{2,1,0:T(1,128)}), f32[8,1,1]{2,1,0:T(1,128)S(1)}, u32[]{:S(2)}, u32[]{:S(2)}) async-start(f32[8,1,1]{2,1,0:T(1,128)} %copy.48), calls=%async_computation.1 | async-start | bytes 8192 | tf_op jit(solution)/shard_map/all_to_all | solution.py:52
  190.8 7.5 %all-to-all-done.1 = f32[8,1,1]{2,1,0:T(1,128)S(1)} async-done(((f32[8,1,1]{2,1,0:T(1,128)}), f32[8,1,1]{2,1,0:T(1,128)S(1)}, u32[]{:S(2)}, u32[]{:S(2)}) %all-to-all-start.1) | async-done | bytes 64 | tf_op jit(solution)/shard_map/all_to_all | solution.py:52
  202.4 1.3 multiply_reduce_fusion.1
  205.6 7.1 %all-to-all-start.2 = ((f32[8,1,1]{2,1,0:T(1,128)}), f32[8,1,1]{2,1,0:T(1,128)S(1)}, u32[]{:S(2)}, u32[]{:S(2)}) async-start(f32[8,1,1]{2,1,0:T(1,128)} %broadcast_in_dim.91), calls=%async_computation.2 | async-start | bytes 8192 | tf_op jit(solution)/shard_map/all_to_all | solution.py:58
  213.4 7.0 %all-to-all-done.2 = f32[8,1,1]{2,1,0:T(1,128)S(1)} async-done(((f32[8,1,1]{2,1,0:T(1,128)}), f32[8,1,1]{2,1,0:T(1,128)S(1)}, u32[]{:S(2)}, u32[]{:S(2)}) %all-to-all-start.2) | async-done | bytes 64 | tf_op jit(solution)/shard_map/all_to_all | solution.py:58
  (203 shorter events, 77.2 us)
Async XLA Ops:
  5.2 4.7 %collective-permute-start = (bf16[8,12,1,32]{3,1,0,2:T(8,128)(2,1)S(1)}, bf16[8,12,1,32]{3,1,0,2:T(8,128)(2,1)S(1)}, u32[]{:S(2)}, u32[]{:S(2)}) collective-permute-start(bf16[8,12,1,32]{3,1,0,2:T(8,128)(2,1)S(1)} %slice.1913), channel_id=1, source_target_pairs={{0,1},{1,2},{2,3},{3,4},{4,5},{5,6},{6,7},{7,8},{8,9},{9,10},{10,1... | collective-permute-start | bytes 18440 | tf_op jit(solution)/shard_map/ppermute | solution.py:19
  6.9 5.5 %collective-permute-start.1 = (bf16[8,12,1,32]{3,1,0,2:T(8,128)(2,1)S(1)}, bf16[8,12,1,32]{3,1,0,2:T(8,128)(2,1)S(1)}, u32[]{:S(2)}, u32[]{:S(2)}) collective-permute-start(bf16[8,12,1,32]{3,1,0,2:T(8,128)(2,1)S(1)} %slice.1913), channel_id=1, source_target_pairs={{1,0},{2,1},{3,2},{4,3},{5,4},{6,5},{7,6},{8,7},{9,8},{10,9},{11,1... | collective-permute-start | bytes 18440 | tf_op jit(solution)/shard_map/ppermute | solution.py:20
  17.3 7.7 %collective-permute-start.2 = (bf16[8,1,32,512]{3,2,0,1:T(8,128)(2,1)S(1)}, bf16[8,1,32,512]{3,2,0,1:T(8,128)(2,1)S(1)}, u32[]{:S(2)}, u32[]{:S(2)}) collective-permute-start(bf16[8,1,32,512]{3,2,0,1:T(8,128)(2,1)S(1)} %bitcast.923), channel_id=1, source_target_pairs={{0,1},{1,2},{2,3},{3,4},{4,5},{5,6},{6,7},{7,8},{8,9},{9,10},{10,1... | collective-permute-start | bytes 786440 | tf_op jit(solution)/shard_map/ppermute | solution.py:19
  22.8 3.4 %collective-permute-start.3 = (bf16[8,1,32,512]{3,2,0,1:T(8,128)(2,1)S(1)}, bf16[8,1,32,512]{3,2,0,1:T(8,128)(2,1)S(1)}, u32[]{:S(2)}, u32[]{:S(2)}) collective-permute-start(bf16[8,1,32,512]{3,2,0,1:T(8,128)(2,1)S(1)} %bitcast.924), channel_id=1, source_target_pairs={{1,0},{2,1},{3,2},{4,3},{5,4},{6,5},{7,6},{8,7},{9,8},{10,9},{11,1... | collective-permute-start | bytes 786440 | tf_op jit(solution)/shard_map/ppermute | solution.py:20
  36.4 13.9 %collective-permute-start.4 = (bf16[8,12,1,32]{3,1,0,2:T(8,128)(2,1)S(1)}, bf16[8,12,1,32]{3,1,0,2:T(8,128)(2,1)S(1)}, u32[]{:S(2)}, u32[]{:S(2)}) collective-permute-start(bf16[8,12,1,32]{3,1,0,2:T(8,128)(2,1)S(1)} %slice.1912), channel_id=1, source_target_pairs={{0,1},{1,2},{2,3},{3,4},{4,5},{5,6},{6,7},{7,8},{8,9},{9,10},{10,1... | collective-permute-start | bytes 18440 | tf_op jit(solution)/shard_map/ppermute | solution.py:19
  49.0 3.1 %collective-permute-start.5 = (bf16[8,12,1,32]{3,1,0,2:T(8,128)(2,1)S(1)}, bf16[8,12,1,32]{3,1,0,2:T(8,128)(2,1)S(1)}, u32[]{:S(2)}, u32[]{:S(2)}) collective-permute-start(bf16[8,12,1,32]{3,1,0,2:T(8,128)(2,1)S(1)} %slice.1912), channel_id=1, source_target_pairs={{1,0},{2,1},{3,2},{4,3},{5,4},{6,5},{7,6},{8,7},{9,8},{10,9},{11,1... | collective-permute-start | bytes 18440 | tf_op jit(solution)/shard_map/ppermute | solution.py:20
  55.0 8.4 %collective-permute-start.6 = (bf16[8,1,32,512]{3,2,0,1:T(8,128)(2,1)S(1)}, bf16[8,1,32,512]{3,2,0,1:T(8,128)(2,1)S(1)}, u32[]{:S(2)}, u32[]{:S(2)}) collective-permute-start(bf16[8,1,32,512]{3,2,0,1:T(8,128)(2,1)S(1)} %bitcast.926), channel_id=1, source_target_pairs={{0,1},{1,2},{2,3},{3,4},{4,5},{5,6},{6,7},{7,8},{8,9},{9,10},{10,1... | collective-permute-start | bytes 786440 | tf_op jit(solution)/shard_map/ppermute | solution.py:19
  61.2 3.4 %collective-permute-start.7 = (bf16[8,1,32,512]{3,2,0,1:T(8,128)(2,1)S(1)}, bf16[8,1,32,512]{3,2,0,1:T(8,128)(2,1)S(1)}, u32[]{:S(2)}, u32[]{:S(2)}) collective-permute-start(bf16[8,1,32,512]{3,2,0,1:T(8,128)(2,1)S(1)} %bitcast.927), channel_id=1, source_target_pairs={{1,0},{2,1},{3,2},{4,3},{5,4},{6,5},{7,6},{8,7},{9,8},{10,9},{11,1... | collective-permute-start | bytes 786440 | tf_op jit(solution)/shard_map/ppermute | solution.py:20
  74.9 10.4 %collective-permute-start.8 = (bf16[8,12,1,32]{3,1,0,2:T(8,128)(2,1)S(1)}, bf16[8,12,1,32]{3,1,0,2:T(8,128)(2,1)S(1)}, u32[]{:S(2)}, u32[]{:S(2)}) collective-permute-start(bf16[8,12,1,32]{3,1,0,2:T(8,128)(2,1)S(1)} %slice.1916), channel_id=1, source_target_pairs={{0,1},{1,2},{2,3},{3,4},{4,5},{5,6},{6,7},{7,8},{8,9},{9,10},{10,1... | collective-permute-start | bytes 18440 | tf_op jit(solution)/shard_map/ppermute | solution.py:19
  83.3 3.1 %collective-permute-start.9 = (bf16[8,12,1,32]{3,1,0,2:T(8,128)(2,1)S(1)}, bf16[8,12,1,32]{3,1,0,2:T(8,128)(2,1)S(1)}, u32[]{:S(2)}, u32[]{:S(2)}) collective-permute-start(bf16[8,12,1,32]{3,1,0,2:T(8,128)(2,1)S(1)} %slice.1916), channel_id=1, source_target_pairs={{1,0},{2,1},{3,2},{4,3},{5,4},{6,5},{7,6},{8,7},{9,8},{10,9},{11,1... | collective-permute-start | bytes 18440 | tf_op jit(solution)/shard_map/ppermute | solution.py:20
  89.3 7.8 %collective-permute-start.10 = (bf16[8,1,32,512]{3,2,0,1:T(8,128)(2,1)S(1)}, bf16[8,1,32,512]{3,2,0,1:T(8,128)(2,1)S(1)}, u32[]{:S(2)}, u32[]{:S(2)}) collective-permute-start(bf16[8,1,32,512]{3,2,0,1:T(8,128)(2,1)S(1)} %bitcast.929), channel_id=1, source_target_pairs={{0,1},{1,2},{2,3},{3,4},{4,5},{5,6},{6,7},{7,8},{8,9},{9,10},{10,1... | collective-permute-start | bytes 786440 | tf_op jit(solution)/shard_map/ppermute | solution.py:19
  95.8 3.4 %collective-permute-start.11 = (bf16[8,1,32,512]{3,2,0,1:T(8,128)(2,1)S(1)}, bf16[8,1,32,512]{3,2,0,1:T(8,128)(2,1)S(1)}, u32[]{:S(2)}, u32[]{:S(2)}) collective-permute-start(bf16[8,1,32,512]{3,2,0,1:T(8,128)(2,1)S(1)} %bitcast.930), channel_id=1, source_target_pairs={{1,0},{2,1},{3,2},{4,3},{5,4},{6,5},{7,6},{8,7},{9,8},{10,9},{11,1... | collective-permute-start | bytes 786440 | tf_op jit(solution)/shard_map/ppermute | solution.py:20
  105.9 39.8 %copy-start.3 = (bf16[2,9,24,512]{3,2,1,0:T(8,128)(2,1)S(1)}, bf16[2,9,24,512]{3,2,1,0:T(8,128)(2,1)}, u32[]{:S(2)}) copy-start(bf16[2,9,24,512]{3,2,1,0:T(8,128)(2,1)} %param.40) | copy-start | bytes 1327108
  111.0 23.0 %all-to-all-start = ((f32[8,1,384]{2,1,0:T(1,128)}), f32[8,1,384]{2,1,0:T(1,128)S(1)}, u32[]{:S(2)}, u32[]{:S(2)}) async-start(f32[8,1,384]{2,1,0:T(1,128)} %reshape.1494), calls=%async_computation | async-start | bytes 24576 | tf_op jit(solution)/shard_map/all_to_all | solution.py:228
  135.5 5.6 %collective-permute-start.12 = (bf16[1,24,1,16]{1,3,2,0:T(8,128)(2,1)S(1)}, bf16[1,24,1,16]{1,3,2,0:T(8,128)(2,1)S(1)}, u32[]{:S(2)}, u32[]{:S(2)}) collective-permute-start(bf16[1,24,1,16]{1,3,2,0:T(8,128)(2,1)S(1)} %get-tuple-element.52), channel_id=1, source_target_pairs={{0,8},{8,16},{16,24},{24,32},{32,40},{40,48},{48,56},{1,9},{9,17},... | collective-permute-start | bytes 2312 | tf_op jit(solution)/shard_map/ppermute | solution.py:36
  139.8 5.9 %collective-permute-start.13 = (bf16[1,24,1,16]{1,3,2,0:T(8,128)(2,1)S(1)}, bf16[1,24,1,16]{1,3,2,0:T(8,128)(2,1)S(1)}, u32[]{:S(2)}, u32[]{:S(2)}) collective-permute-start(bf16[1,24,1,16]{1,3,2,0:T(8,128)(2,1)S(1)} %get-tuple-element.53), channel_id=1, source_target_pairs={{8,0},{16,8},{24,16},{32,24},{40,32},{48,40},{56,48},{9,1},{17,9},... | collective-permute-start | bytes 2312 | tf_op jit(solution)/shard_map/ppermute | solution.py:39
  147.2 16.8 %collective-permute-start.14 = (bf16[1,1,16,512]{3,2,1,0:T(8,128)(2,1)S(1)}, bf16[1,1,16,512]{3,2,1,0:T(8,128)(2,1)S(1)}, u32[]{:S(2)}, u32[]{:S(2)}) collective-permute-start(bf16[1,1,16,512]{3,2,1,0:T(8,128)(2,1)S(1)} %get-tuple-element.42), channel_id=1, source_target_pairs={{0,8},{8,16},{16,24},{24,32},{32,40},{40,48},{48,56},{1,9},{9,17},... | collective-permute-start | bytes 49160 | tf_op jit(solution)/shard_map/ppermute | solution.py:36
  161.2 5.6 %collective-permute-start.15 = (bf16[1,1,16,512]{3,2,1,0:T(8,128)(2,1)S(1)}, bf16[1,1,16,512]{3,2,1,0:T(8,128)(2,1)S(1)}, u32[]{:S(2)}, u32[]{:S(2)}) collective-permute-start(bf16[1,1,16,512]{3,2,1,0:T(8,128)(2,1)S(1)} %get-tuple-element.43), channel_id=1, source_target_pairs={{8,0},{16,8},{24,16},{32,24},{40,32},{48,40},{56,48},{9,1},{17,9},... | collective-permute-start | bytes 49160 | tf_op jit(solution)/shard_map/ppermute | solution.py:39
  169.2 10.2 %collective-permute-start.16 = (bf16[1,24,1,16]{1,3,2,0:T(8,128)(2,1)S(1)}, bf16[1,24,1,16]{1,3,2,0:T(8,128)(2,1)S(1)}, u32[]{:S(2)}, u32[]{:S(2)}) collective-permute-start(bf16[1,24,1,16]{1,3,2,0:T(8,128)(2,1)S(1)} %get-tuple-element.50), channel_id=1, source_target_pairs={{0,8},{8,16},{16,24},{24,32},{32,40},{40,48},{48,56},{1,9},{9,17},... | collective-permute-start | bytes 2312 | tf_op jit(solution)/shard_map/ppermute | solution.py:36
  173.1 6.3 %collective-permute-start.17 = (bf16[1,24,1,16]{1,3,2,0:T(8,128)(2,1)S(1)}, bf16[1,24,1,16]{1,3,2,0:T(8,128)(2,1)S(1)}, u32[]{:S(2)}, u32[]{:S(2)}) collective-permute-start(bf16[1,24,1,16]{1,3,2,0:T(8,128)(2,1)S(1)} %get-tuple-element.51), channel_id=1, source_target_pairs={{8,0},{16,8},{24,16},{32,24},{40,32},{48,40},{56,48},{9,1},{17,9},... | collective-permute-start | bytes 2312 | tf_op jit(solution)/shard_map/ppermute | solution.py:39
  181.0 18.7 %collective-permute-start.18 = (bf16[1,1,16,512]{3,2,1,0:T(8,128)(2,1)S(1)}, bf16[1,1,16,512]{3,2,1,0:T(8,128)(2,1)S(1)}, u32[]{:S(2)}, u32[]{:S(2)}) collective-permute-start(bf16[1,1,16,512]{3,2,1,0:T(8,128)(2,1)S(1)} %get-tuple-element.40), channel_id=1, source_target_pairs={{0,8},{8,16},{16,24},{24,32},{32,40},{40,48},{48,56},{1,9},{9,17},... | collective-permute-start | bytes 49160 | tf_op jit(solution)/shard_map/ppermute | solution.py:36
  185.5 14.1 %collective-permute-start.19 = (bf16[1,1,16,512]{3,2,1,0:T(8,128)(2,1)S(1)}, bf16[1,1,16,512]{3,2,1,0:T(8,128)(2,1)S(1)}, u32[]{:S(2)}, u32[]{:S(2)}) collective-permute-start(bf16[1,1,16,512]{3,2,1,0:T(8,128)(2,1)S(1)} %get-tuple-element.41), channel_id=1, source_target_pairs={{8,0},{16,8},{24,16},{32,24},{40,32},{48,40},{56,48},{9,1},{17,9},... | collective-permute-start | bytes 49160 | tf_op jit(solution)/shard_map/ppermute | solution.py:39
  187.5 10.9 %all-to-all-start.1 = ((f32[8,1,1]{2,1,0:T(1,128)}), f32[8,1,1]{2,1,0:T(1,128)S(1)}, u32[]{:S(2)}, u32[]{:S(2)}) async-start(f32[8,1,1]{2,1,0:T(1,128)} %copy.48), calls=%async_computation.1 | async-start | bytes 8192 | tf_op jit(solution)/shard_map/all_to_all | solution.py:52
  205.6 14.8 %all-to-all-start.2 = ((f32[8,1,1]{2,1,0:T(1,128)}), f32[8,1,1]{2,1,0:T(1,128)S(1)}, u32[]{:S(2)}, u32[]{:S(2)}) async-start(f32[8,1,1]{2,1,0:T(1,128)} %broadcast_in_dim.91), calls=%async_computation.2 | async-start | bytes 8192 | tf_op jit(solution)/shard_map/all_to_all | solution.py:58
  (14 other events, 234.3 us)
where the time goes:
time: 226 us; the launch traced here: 223 us
  starting transfers between devices  106 us (47%)
  matrix products  47.6 us (21%)
  waiting for transfers between devices  39.3 us (17%)
  between operations  12.5 us (6%)
  other arithmetic  11.4 us (5%)
  local copies, waits for them, and re-layouts  5.92 us (3%)
    ppermute x6, starting transfers between devices, padded_2(): lax.ppermute(last, axis, up)  40.8 us
    dot_general x45, matrix products, conv_out(): jnp.einsum('bhwc,co->bohw', window, weights[tap_idx], preferred_element_t...  30.4 us
    ppermute x4, starting transfers between devices, with_halo(): lax.ppermute(lax.slice_in_dim(block, block.shape[dim] - width, None, axis...  26.7 us
    all_to_all x1, starting transfers between devices, body(): lax.all_to_all(kept_chan, 'chan', split_axis=0, concat_axis=2, tiled=True)  15.3 us
    dot_general x40, matrix products, conv_in(): jnp.einsum('bchw,co->bhwo', window, weights[tap_idx], preferred_element_t...  10.6 us
    ppermute x6, waiting for transfers between devices, padded_2(): lax.ppermute(first, axis, [(b, a) for a, b in up])  9.81 us
    ppermute x6, starting transfers between devices, padded_2(): lax.ppermute(first, axis, [(b, a) for a, b in up])  7.75 us
    all_to_all x1, waiting for transfers between devices, summed_on_arrival(): pieces = lax.all_to_all(in_blocks(x, dim, length), axis, 0, 0, tiled=True)  7.54 us
  transfers between devices with their start and end apart: 23, of which 11 were waited for; matrix products, arithmetic and copies ran while one was open for 3% of the time, Pallas kernels for 0%

commit v1 on v0

v1 whole, which is shorter than its diff:
```python
import functools
import math

import jax
import jax.numpy as jnp
from jax import lax
from jax.experimental import pallas as pl
from jax.experimental.pallas import tpu as pltpu
from jax.sharding import PartitionSpec as P

MESH = pl.DeviceIdType.MESH
F32 = jnp.float32
BF16 = jnp.bfloat16
HI = lax.Precision.HIGHEST
log_two_pi = math.log(2.0 * math.pi)


def iota2(shape, dim):
    return lax.broadcasted_iota(jnp.int32, shape, dim)


def mixing(lower, upper, diag, gain, shift, spread, place, split_at):
    n = lower.shape[0]
    r, c = iota2((n, n), 0), iota2((n, n), 1)
    low = jnp.where(r > c, lower, jnp.where(r == c, 1.0, 0.0))
    up = jnp.where(c > r, upper, jnp.where(r == c, jnp.exp(diag), 0.0)) * jnp.exp(gain)
    both = jnp.dot(low, up, precision=HI, preferred_element_type=F32)
    if spread is not None:
        both = jnp.dot(spread, both, precision=HI, preferred_element_type=F32)
    const = jnp.sum(both * shift, axis=1, keepdims=True)
    wide = jnp.dot(both, place, precision=HI, preferred_element_type=F32)
    high = wide.astype(BF16).astype(F32)
    lane = iota2(wide.shape, 1)
    return jnp.where(lane < split_at, high, wide - high).astype(BF16), const


def column(row):
    n = row.shape[1]
    eye = iota2((n, n), 0) == iota2((n, n), 1)
    return jnp.sum(jnp.where(eye, jnp.broadcast_to(row, (n, n)), 0.0), axis=1, keepdims=True)


def apply_mix(state, mix, const):
    high = state.astype(BF16)
    low = (state - high.astype(F32)).astype(BF16)
    stacked = jnp.concatenate([high, low, high], axis=0)
    return jnp.dot(mix, stacked, preferred_element_type=F32) + const


def coupling(u, half, pad, w1t, w2t, bias2, w3, bias3, left_ok, right_ok, up_ok, down_ok, cols, tile, extra):
    length = u.shape[1]
    ua, ub = u[:pad], u[pad : 2 * pad]
    q = ua.astype(BF16).astype(F32)
    sides = (
        jnp.where(left_ok, pltpu.roll(q, 1, 1), 0.0),
        q,
        jnp.where(right_ok, pltpu.roll(q, length - 1, 1), 0.0),
    )
    above = [jnp.where(up_ok, pltpu.roll(s, cols, 1), 0.0) for s in sides]
    below = [jnp.where(down_ok, pltpu.roll(s, length - cols, 1), 0.0) for s in sides]
    stack = [*above, *sides, *below]
    if extra:
        stack.append(jnp.ones((8, length), F32))
    patches = jnp.concatenate(stack, axis=0).astype(BF16)
    pieces = []
    for at in range(0, length, tile):
        h = jnp.dot(w1t[...], patches[:, at : at + tile], preferred_element_type=F32)
        h = jnp.maximum(h, 0.0).astype(BF16)
        h = jnp.dot(w2t[...], h, preferred_element_type=F32)
        b = bias2[...]
        b = jnp.concatenate([b] * (tile // 128), axis=1)
        h = jnp.maximum(h + b, 0.0).astype(BF16)
        pieces.append(jnp.dot(w3[...], h, preferred_element_type=F32))
    taps = jnp.concatenate(pieces, axis=1) if len(pieces) > 1 else pieces[0]
    both = 2 * half
    rows = []
    for dr in range(3):
        a, b, c = (taps[(dr * 3 + dc) * both : (dr * 3 + dc + 1) * both] for dc in range(3))
        rows.append(
            b
            + jnp.where(left_ok, pltpu.roll(a, 1, 1), 0.0)
            + jnp.where(right_ok, pltpu.roll(c, length - 1, 1), 0.0)
        )
    out = (
        rows[1]
        + jnp.where(up_ok, pltpu.roll(rows[0], cols, 1), 0.0)
        + jnp.where(down_ok, pltpu.roll(rows[2], length - cols, 1), 0.0)
        + bias3
    )
    g, t = out[:half] + 2.0, out[half:]
    if pad > half:
        zeros = jnp.zeros((pad - half, length), F32)
        g, t = jnp.concatenate([g, zeros], axis=0), jnp.concatenate([t, zeros], axis=0)
    return ua, (ub + t) * jax.nn.sigmoid(g), g


def log_sigmoid(g):
    return jnp.minimum(g, 0.0) - jnp.log1p(jnp.exp(-jnp.abs(g)))


def kernel(
    n_rows,
    n_chan,
    images,
    shift_mid,
    gain_mid,
    lower_mid,
    upper_mid,
    diag_mid,
    first_mid,
    first_bias_mid,
    second_mid,
    second_bias_mid,
    third_mid,
    third_bias_mid,
    shift_top,
    gain_top,
    lower_top,
    upper_top,
    diag_top,
    first_top,
    first_bias_top,
    second_top,
    second_bias_top,
    third_top,
    third_bias_top,
    latent_mid,
    latent_top,
    loglik,
    img_v,
    w1m,
    w2m,
    w3m,
    w1p,
    w2p,
    w3p,
    w1f_m,
    w1f_p,
    w1m_t,
    w2m_t,
    w1p_t,
    w2p_t,
    b2m,
    b2p,
    mix_m,
    mix_p0,
    mix_p1,
    const_m,
    const_p,
    y_out,
    y_in,
    z_out,
    z_in,
    back_out,
    back_in,
    ll_out,
    ll_in,
    load_sem,
    ys_sem,
    yr_sem,
    zs_sem,
    zr_sem,
    bs_sem,
    br_sem,
    ls_sem,
    lr_sem,
):
    me_row, me_chan = lax.axis_index("rows"), lax.axis_index("chan")
    steps_m, steps_p = shift_mid.shape[0], shift_top.shape[0]
    n_img, c_mid, width = img_v.shape
    half_m = c_mid // 2
    c_top = shift_top.shape[1]
    half_p = c_top // 2

    loads = [
        pltpu.make_async_copy(src, dst, load_sem.at[k])
        for k, (src, dst) in enumerate(
            (
                (images, img_v),
                (first_mid, w1m),
                (second_mid, w2m),
                (third_mid, w3m),
                (first_top, w1p),
                (second_top, w2p),
                (third_top, w3p),
            )
        )
    ]
    for load in loads:
        load.start()

    barrier = pltpu.get_barrier_semaphore()
    chan_peers = [lax.rem(me_chan + k, n_chan) for k in range(1, n_chan)]
    row_peers = [lax.rem(me_row + k, n_rows) for k in range(1, n_rows)]
    for peer in chan_peers:
        pl.semaphore_signal(barrier, inc=1, device_id={"chan": peer}, device_id_type=MESH)
    for peer in row_peers:
        pl.semaphore_signal(barrier, inc=1, device_id={"rows": peer}, device_id_type=MESH)

    loads[0].wait()
    for i in range(n_img):
        row = img_v[i]
        packed = [row[8 * k : 8 * k + 8] for k in range(c_mid // 8)]
        packed.append(jnp.zeros((8, 128 - width * (c_mid // 8)), F32))
        y_out[i] = jnp.concatenate(packed, axis=1)
    y_in[me_chan] = y_out[me_chan]

    spread = jnp.where(
        iota2((32, c_mid), 0)
        == iota2((32, c_mid), 1) + jnp.where(iota2((32, c_mid), 1) >= half_m, 16 - half_m, 0),
        1.0,
        0.0,
    )
    src, lane = iota2((c_mid, 96), 0), lax.rem(iota2((c_mid, 96), 1), 32)
    plain = jnp.where(src == lane, 1.0, 0.0)
    padded = jnp.where(src + jnp.where(src >= half_m, 16 - half_m, 0) == lane, 1.0, 0.0)
    for s in range(steps_m):
        mix, const = mixing(
            lower_mid[s],
            upper_mid[s],
            diag_mid[s : s + 1],
            gain_mid[s : s + 1],
            shift_mid[s : s + 1],
            spread,
            plain if s == 0 else padded,
            64,
        )
        mix_m[s] = mix
        const_m[s] = jnp.where(iota2((32, 1), 0) == half_m, 1.0, const)
    src, lane = iota2((c_top, 192), 0), lax.rem(iota2((c_top, 192), 1), 64)
    squeezed_place = jnp.where(
        jnp.logical_and(lax.rem(lane, 16) < half_m, src == 4 * lax.rem(lane, 16) + lax.div(lane, 16)), 1.0, 0.0
    )
    src, lane = iota2((c_top, 144), 0), lax.rem(iota2((c_top, 144), 1), 48)
    top_place = jnp.where(src == lane, 1.0, 0.0)
    for s in range(steps_p):
        mix, const = mixing(
            lower_top[s],
            upper_top[s],
            diag_top[s : s + 1],
            gain_top[s : s + 1],
            shift_top[s : s + 1],
            None,
            squeezed_place if s == 0 else top_place,
            128 if s == 0 else 96,
        )
        if s == 0:
            mix_p0[...] = mix
        else:
            mix_p1[s - 1] = mix
        const_p[s] = const

    pl.semaphore_wait(barrier, n_chan + n_rows - 2)
    y_copies = []
    for k, peer in enumerate(chan_peers):
        copy = pltpu.make_async_remote_copy(
            src_ref=y_out.at[peer],
            dst_ref=y_in.at[me_chan],
            send_sem=ys_sem.at[k],
            recv_sem=yr_sem.at[n_chan - 2 - k],
            device_id={"chan": peer},
            device_id_type=MESH,
        )
        copy.start()
        y_copies.append(copy)

    def prepare_mid(s):
        w1f_m[...] = jnp.zeros_like(w1f_m)
        for t in range(9):
            w1f_m[16 * t : 16 * t + half_m] = w1m[s, t].astype(F32)
        w1f_m[64 + half_m : 65 + half_m] = first_bias_mid[s : s + 1].astype(F32)
        w1m_t[s] = w1f_m[...].T.astype(BF16)
        w2m_t[s] = w2m[s].T
        b2m[s] = jnp.broadcast_to(second_bias_mid[s : s + 1], (128, b2m.shape[1])).T

    def prepare_top(s):
        w1f_p[9 * half_p :] = jnp.zeros((8, w1f_p.shape[1]), F32)
        w1f_p[: 9 * half_p] = w1p[s].astype(F32)
        w1f_p[9 * half_p : 9 * half_p + 1] = first_bias_top[s : s + 1].astype(F32)
        w1p_t[s] = w1f_p[...].T.astype(BF16)
        w2p_t[s] = w2p[s].T
        b2p[s] = jnp.broadcast_to(second_bias_top[s : s + 1], (128, b2p.shape[1])).T

    loads[1].wait()
    loads[2].wait()
    prepare_mid(0)

    for copy in y_copies:
        copy.wait_recv()
    groups = []
    for k in range(c_mid // 8):
        groups.append(jnp.concatenate([y_in[c][:, width * k : width * (k + 1)] for c in range(n_chan)], axis=1))
    own = jnp.concatenate([*groups, jnp.zeros((32 - c_mid, n_chan * width), F32)], axis=0)
    z_out[...] = own.astype(BF16)
    z_copies = []
    for k, d in enumerate((1, -1, 2, -2)):
        copy = pltpu.make_async_remote_copy(
            src_ref=z_out,
            dst_ref=z_in.at[k],
            send_sem=zs_sem.at[k],
            recv_sem=zr_sem.at[k],
            device_id={"rows": lax.rem(me_row + d + n_rows, n_rows)},
            device_id_type=MESH,
        )
        copy.start()
        z_copies.append(copy)
    for s in range(1, steps_m):
        prepare_mid(s)
    for load in loads[3:]:
        load.wait()
    for s in range(steps_p):
        prepare_top(s)
    bias3_m = [column(third_bias_mid[s : s + 1]) for s in range(steps_m)]
    bias3_p = [column(third_bias_top[s : s + 1]) for s in range(steps_p)]
    for copy in z_copies:
        copy.wait_recv()
    state = jnp.concatenate([z_in[2].astype(F32), z_in[0].astype(F32), own, z_in[1].astype(F32), z_in[3].astype(F32)], axis=1)

    height = n_rows * n_chan
    partial = jnp.zeros((8, 128), F32)

    def folded(x):
        total = None
        for i in range(0, x.shape[0], 8):
            for j in range(0, x.shape[1], 128):
                piece = x[i : i + 8, j : j + 128]
                total = piece if total is None else total + piece
        return total

    first_row = me_row * n_chan - 2 * n_chan
    own_at = 2 * n_chan * width
    own_lanes = n_chan * width
    valid_m = iota2((16, own_lanes), 0) < half_m
    for s in range(steps_m):
        if s == 1:
            state = state[:, 4 * width : 36 * width]
            first_row = first_row + 4
            own_at = own_at - 4 * width
        length = state.shape[1]
        lane = iota2((1, length), 1)
        col, row = lax.rem(lane, width), lax.div(lane, width) + first_row
        u = apply_mix(state, mix_m[s], const_m[s])
        ua, updated, g = coupling(
            u,
            half_m,
            16,
            w1m_t.at[s],
            w2m_t.at[s],
            b2m.at[s],
            w3m.at[s],
            bias3_m[s],
            col >= 1,
            col <= width - 2,
            row >= 1,
            row <= height - 2,
            width,
            256,
            False,
        )
        state = jnp.concatenate([ua, updated], axis=0)
        mine = g[:, own_at : own_at + own_lanes]
        partial = partial + folded(jnp.where(valid_m, log_sigmoid(mine), 0.0))
    latent = jnp.where(valid_m, state[:16, own_at : own_at + own_lanes], 0.0)
    partial = partial + folded(-0.5 * latent * latent)

    for c in range(n_chan):
        piece = latent[:, width * c : width * (c + 1)]
        back_out[c] = jnp.concatenate([piece[:8], piece[8:], jnp.zeros((8, 128 - 2 * width), F32)], axis=1)
    back_in[me_chan] = back_out[me_chan]
    back_copies = []
    for k, peer in enumerate(chan_peers):
        copy = pltpu.make_async_remote_copy(
            src_ref=back_out.at[peer],
            dst_ref=back_in.at[me_chan],
            send_sem=bs_sem.at[k],
            recv_sem=br_sem.at[n_chan - 2 - k],
            device_id={"chan": peer},
            device_id_type=MESH,
        )
        copy.start()
        back_copies.append(copy)

    kept = state[16:, 4 * width : 28 * width]
    cols_p = width // 2
    lane = iota2((16, 128), 1)
    phase, rest = lax.div(lane, 32), lax.rem(lane, 32)
    pick = (2 * lax.div(rest, cols_p) + lax.div(phase, 2)) * width + 2 * lax.rem(rest, cols_p) + lax.rem(phase, 2)
    blocks = [
        jnp.take_along_axis(kept[:, 128 * k : 128 * k + 128], pick, axis=1) for k in range(kept.shape[1] // 128)
    ]
    phases = []
    for p in range(4):
        parts = [b[:, 32 * p : 32 * p + 32] for b in blocks]
        parts.append(jnp.zeros((16, 256 - 32 * len(blocks)), F32))
        phases.append(jnp.concatenate(parts, axis=1))
    state = jnp.concatenate(phases, axis=0)

    rows_p = n_chan // 2
    first_row = me_row * rows_p - rows_p
    length = state.shape[1]
    lane = iota2((1, length), 1)
    col, row = lax.rem(lane, cols_p), lax.div(lane, cols_p) + first_row
    own_at = rows_p * cols_p
    mine_p = jnp.logical_and(lane >= own_at, lane < 2 * own_at)
    for s in range(steps_p):
        u = apply_mix(state, mix_p0[...] if s == 0 else mix_p1[s - 1], const_p[s])
        ua, updated, g = coupling(
            u,
            half_p,
            half_p,
            w1p_t.at[s],
            w2p_t.at[s],
            b2p.at[s],
            w3p.at[s],
            bias3_p[s],
            col >= 1,
            col <= cols_p - 2,
            row >= 1,
            row <= height // 2 - 2,
            cols_p,
            256,
            True,
        )
        state = jnp.concatenate([ua, updated], axis=0)
        partial = partial + folded(jnp.where(mine_p, log_sigmoid(g), 0.0))
    partial = partial + folded(jnp.where(mine_p, -0.5 * state * state, 0.0))
    ll_out[...] = jnp.sum(partial, axis=0, keepdims=True)
    ll_copies = []
    for k, peer in enumerate(row_peers):
        copy = pltpu.make_async_remote_copy(
            src_ref=ll_out,
            dst_ref=ll_in.at[n_rows - 2 - k],
            send_sem=ls_sem.at[k],
            recv_sem=lr_sem.at[n_rows - 2 - k],
            device_id={"rows": peer},
            device_id_type=MESH,
        )
        copy.start()
        ll_copies.append(copy)

    latent_top[...] = state[:, :128].T[own_at : 2 * own_at]
    for copy in back_copies:
        copy.wait_recv()
    for c in range(n_img):
        piece = back_in[c]
        latent_mid[c, :8] = piece[:, :width]
        latent_mid[c, 8:half_m] = piece[: half_m - 8, width : 2 * width]
    cells = height * width
    const = sum(
        (
            cells * (jnp.sum(gain_mid[...]) + jnp.sum(diag_mid[...])),
            (cells // 4) * (jnp.sum(gain_top[...]) + jnp.sum(diag_top[...])),
        )
    )
    for copy in ll_copies:
        copy.wait_recv()
    total = ll_out[...]
    for k in range(n_rows - 1):
        total = total + ll_in[k]
    scale = 1.0 / (c_mid * cells)
    loglik[...] = jnp.broadcast_to((jnp.sum(total) + const) * scale - 0.5 * log_two_pi, (1, 128))
    for copy in (*y_copies, *z_copies, *back_copies, *ll_copies):
        copy.wait_send()


def body(
    images,
    shift_mid,
    gain_mid,
    lower_mid,
    upper_mid,
    diag_mid,
    first_mid,
    first_bias_mid,
    second_mid,
    second_bias_mid,
    third_mid,
    third_bias_mid,
    shift_top,
    gain_top,
    lower_top,
    upper_top,
    diag_top,
    first_top,
    first_bias_top,
    second_top,
    second_bias_top,
    third_top,
    third_bias_top,
):
    n_rows, n_chan = lax.axis_size("rows"), lax.axis_size("chan")
    n_img, c_mid, _, width = images.shape
    hid = second_mid.shape[1]
    steps_m, steps_p = shift_mid.shape[0], shift_top.shape[0]
    c_top = shift_top.shape[1]
    half_m, half_p = c_mid // 2, c_top // 2
    images = images.reshape(n_img, c_mid, width)
    third_mid = third_mid.transpose(0, 1, 3, 2).reshape(steps_m, 9 * c_mid, hid)
    third_top = third_top.transpose(0, 1, 3, 2).reshape(steps_p, 9 * c_top, hid)
    first_top = first_top.reshape(steps_p, 9 * half_p, hid)
    big = pl.BlockSpec(memory_space=pl.ANY)
    small = pl.BlockSpec(memory_space=pltpu.VMEM)
    where = [big] + [small] * 5 + [big, small] * 2 + [big, small] + [small] * 5 + [big, small] * 3
    rows_p = n_chan // 2
    vmem = pltpu.VMEM
    dma = pltpu.SemaphoreType.DMA
    latent_mid, latent_top, loglik = pl.pallas_call(
        functools.partial(kernel, n_rows, n_chan),
        out_shape=(
            jax.ShapeDtypeStruct((n_img, half_m, width), F32),
            jax.ShapeDtypeStruct((rows_p * width // 2, c_top), F32),
            jax.ShapeDtypeStruct((1, 128), F32),
        ),
        in_specs=where,
        out_specs=(small, small, small),
        scratch_shapes=[
            vmem((n_img, c_mid, width), F32),
            vmem((steps_m, 9, half_m, hid), BF16),
            vmem((steps_m, hid, hid), BF16),
            vmem((steps_m, 9 * c_mid, hid), BF16),
            vmem((steps_p, 9 * half_p, hid), BF16),
            vmem((steps_p, hid, hid), BF16),
            vmem((steps_p, 9 * c_top, hid), BF16),
            vmem((144, hid), F32),
            vmem((9 * half_p + 8, hid), F32),
            vmem((steps_m, hid, 144), BF16),
            vmem((steps_m, hid, hid), BF16),
            vmem((steps_p, hid, 9 * half_p + 8), BF16),
            vmem((steps_p, hid, hid), BF16),
            vmem((steps_m, hid, 128), F32),
            vmem((steps_p, hid, 128), F32),
            vmem((steps_m, 32, 96), BF16),
            vmem((c_top, 192), BF16),
            vmem((steps_p - 1, c_top, 144), BF16),
            vmem((steps_m, 32, 1), F32),
            vmem((steps_p, c_top, 1), F32),
            vmem((n_chan, 8, 128), F32),
            vmem((n_chan, 8, 128), F32),
            vmem((32, n_chan * width), BF16),
            vmem((4, 32, n_chan * width), BF16),
            vmem((n_chan, 8, 128), F32),
            vmem((n_chan, 8, 128), F32),
            vmem((1, 128), F32),
            vmem((n_rows - 1, 1, 128), F32),
            dma((7,)),
            dma((n_chan - 1,)),
            dma((n_chan - 1,)),
            dma((4,)),
            dma((4,)),
            dma((n_chan - 1,)),
            dma((n_chan - 1,)),
            dma((n_rows - 1,)),
            dma((n_rows - 1,)),
        ],
        compiler_params=pltpu.CompilerParams(
            collective_id=0, has_side_effects=True, vmem_limit_bytes=66 * 1000 * 1000
        ),
    )(
        images,
        shift_mid,
        gain_mid,
        lower_mid,
        upper_mid,
        diag_mid,
        first_mid,
        first_bias_mid,
        second_mid,
        second_bias_mid,
        third_mid,
        third_bias_mid,
        shift_top,
        gain_top,
        lower_top,
        upper_top,
        diag_top,
        first_top,
        first_bias_top,
        second_top,
        second_bias_top,
        third_top,
        third_bias_top,
    )
    latent_mid = latent_mid.reshape(n_img, half_m, 1, width)
    latent_top = latent_top.reshape(1, rows_p, width // 2, c_top).transpose(0, 3, 1, 2)
    return latent_mid, latent_top, loglik[0, :1]


def solution(mesh):
    placed = (P("batch", None, ("rows", "chan"), None),) + (P(),) * 22
    return jax.shard_map(
        body,
        mesh=mesh,
        in_specs=placed,
        out_specs=(
            P("batch", None, ("rows", "chan"), None),
            P(("batch", "chan"), None, "rows", None),
            P(("batch", "chan")),
        ),
        check_vma=False,
    )
```

time: 226 us -> 47.8 us (0.21); the launches traced: 223 us -> 47.5 us
  starting transfers between devices: 106 us -> 0 us
  matrix products: 47.6 us -> 0 us
  Pallas kernels: 0 us -> 42.2 us
  waiting for transfers between devices: 39.3 us -> 0 us
  other arithmetic: 11.4 us -> 0 us
  between operations: 12.5 us -> 2.47 us
  local copies, waits for them, and re-layouts: 5.92 us -> 2.88 us
    ppermute x20 -> x0, starting transfers between devices: 80.5 us -> none  [the longest x6 40.8 us: padded_2(): lax.ppermute(last, axis, up)]
    dot_general x100 -> x0, matrix products: 47.6 us -> none  [the longest x45 30.4 us: conv_out(): jnp.einsum('bhwc,co->bohw', window, weights[tap_idx], preferred_element_t...]
    pallas_call x0 -> x1, Pallas kernels: none -> 42.2 us  [body(): pl.pallas_call(functools.partial(kernel, n_rows, n_chan), out_shape=(jax....]
    all_to_all x3 -> x0, starting transfers between devices: 25.7 us -> none  [the longest x1 15.3 us: body(): lax.all_to_all(kept_chan, 'chan', split_axis=0, concat_axis=2, tiled=True)]
    all_to_all x3 -> x0, waiting for transfers between devices: 22.1 us -> none  [the longest x1 7.54 us: summed_on_arrival(): pieces = lax.all_to_all(in_blocks(x, dim, length), axis, 0, 0, tiled=True)]
    ppermute x20 -> x0, waiting for transfers between devices: 17.2 us -> none  [the longest x6 9.81 us: padded_2(): lax.ppermute(first, axis, [(b, a) for a, b in up])]
    reduce_sum x10 -> x0, other arithmetic: 6.51 us -> none  [the longest x2 2.19 us: flow_step(): jnp.sum(diag_log)]
  transfers between devices with their start and end apart: 23 -> 0, of which waited for: 11 -> 0; matrix products, arithmetic and copies ran while one was open for 3% -> 0% of each run, Pallas kernels for 0% -> 0%
where the time goes in v1:
time: 47.8 us; the launch traced here: 47.5 us
  Pallas kernels  42.2 us (88%)
  local copies, waits for them, and re-layouts  2.88 us (6%)
  between operations  2.47 us (5%)
    pallas_call x1, Pallas kernels, body(): pl.pallas_call(functools.partial(kernel, n_rows, n_chan), out_shape=(jax....  42.2 us
    unnamed x2, local copies, waits for them, and re-layouts  2.88 us

profile of v1, /device:TPU:6, one launch (start us, length us, event | category | flops | bytes accessed | tf_op | source)
XLA Modules:
  0.0 47.5 jit_solution(13145209886713051491)
XLA Ops:
  0.6 42.2 %shard_map.238 = (f32[8,12,32]{2,1,0:T(8,128)}, f32[64,48]{1,0:T(8,128)}, f32[1,128]{1,0:T(1,128)}) custom-call(f32[8,24,32]{2,1,0:T(8,128)} %bitcast.17, f32[3,24]{1,0:T(4,128)} %shift_mid.1, f32[3,24]{1,0:T(4,128)} %gain_mid.1, f32[3,24,24]{2,1,0:T(8,128)} %lower_mid.1, f32[3,24,24]{2,1,0:T(8,128)} %upper_mid.1, f32[3,24]{1,0:T(4,128)} %diag_mid.1, ...), custom_call_target="tpu_custom_call" | custom-call | tf_op jit(solution)/shard_map/pallas_call | solution.py:507
  42.8 1.5 %copy.26 = f32[8,12,1,32]{3,2,1,0:T(1,128)} copy(f32[8,12,1,32]{3,1,0,2:T(8,128)} %bitcast.18) | data formatting | bytes 24576
  44.3 1.4 %copy.29 = f32[1,48,4,16]{1,3,2,0:T(8,128)} copy(f32[1,48,4,16]{1,3,2,0:T(8,128)} %bitcast.19) | data formatting | bytes 24576

commit v2 on v1

--- a/solution.py
+++ b/solution.py
@@ -47,6 +47,20 @@
     return jnp.dot(mix, stacked, preferred_element_type=F32) + const
 
 
+def dot(w, x):
+    if x.shape[1] > 256:
+        return jnp.dot(w[...], x, preferred_element_type=F32)
+    rows = w.shape[0]
+    cut = rows // 16 // 2 * 16
+    return jnp.concatenate(
+        [
+            jnp.dot(w[:cut], x, preferred_element_type=F32),
+            jnp.dot(w[cut:], x, preferred_element_type=F32),
+        ],
+        axis=0,
+    )
+
+
 def coupling(u, half, pad, w1t, w2t, bias2, w3, bias3, left_ok, right_ok, up_ok, down_ok, cols, tile, extra):
     length = u.shape[1]
     ua, ub = u[:pad], u[pad : 2 * pad]
@@ -64,13 +78,14 @@
     patches = jnp.concatenate(stack, axis=0).astype(BF16)
     pieces = []
     for at in range(0, length, tile):
-        h = jnp.dot(w1t[...], patches[:, at : at + tile], preferred_element_type=F32)
+        size = min(tile, length - at)
+        h = dot(w1t, patches[:, at : at + size])
         h = jnp.maximum(h, 0.0).astype(BF16)
-        h = jnp.dot(w2t[...], h, preferred_element_type=F32)
+        h = dot(w2t, h)
         b = bias2[...]
-        b = jnp.concatenate([b] * (tile // 128), axis=1)
+        b = jnp.concatenate([b] * (size // 128), axis=1)
         h = jnp.maximum(h + b, 0.0).astype(BF16)
-        pieces.append(jnp.dot(w3[...], h, preferred_element_type=F32))
+        pieces.append(dot(w3, h))
     taps = jnp.concatenate(pieces, axis=1) if len(pieces) > 1 else pieces[0]
     both = 2 * half
     rows = []
@@ -102,28 +117,28 @@
     n_rows,
     n_chan,
     images,
-    shift_mid,
-    gain_mid,
-    lower_mid,
-    upper_mid,
-    diag_mid,
+    shift_mid_h,
+    gain_mid_h,
+    lower_mid_h,
+    upper_mid_h,
+    diag_mid_h,
     first_mid,
-    first_bias_mid,
+    first_bias_mid_h,
     second_mid,
-    second_bias_mid,
+    second_bias_mid_h,
     third_mid,
-    third_bias_mid,
-    shift_top,
-    gain_top,
-    lower_top,
-    upper_top,
-    diag_top,
+    third_bias_mid_h,
+    shift_top_h,
+    gain_top_h,
+    lower_top_h,
+    upper_top_h,
+    diag_top_h,
     first_top,
-    first_bias_top,
+    first_bias_top_h,
     second_top,
-    second_bias_top,
+    second_bias_top_h,
     third_top,
-    third_bias_top,
+    third_bias_top_h,
     latent_mid,
     latent_top,
     loglik,
@@ -155,7 +170,24 @@
     back_in,
     ll_out,
     ll_in,
+    shift_mid,
+    gain_mid,
+    lower_mid,
+    upper_mid,
+    diag_mid,
+    first_bias_mid,
+    second_bias_mid,
+    third_bias_mid,
+    shift_top,
+    gain_top,
+    lower_top,
+    upper_top,
+    diag_top,
+    first_bias_top,
+    second_bias_top,
+    third_bias_top,
     load_sem,
+    small_sem,
     ys_sem,
     yr_sem,
     zs_sem,
@@ -172,6 +204,14 @@
     c_top = shift_top.shape[1]
     half_p = c_top // 2
 
+    barrier = pltpu.get_barrier_semaphore()
+    chan_peers = [lax.rem(me_chan + k, n_chan) for k in range(1, n_chan)]
+    row_peers = [lax.rem(me_row + k, n_rows) for k in range(1, n_rows)]
+    for peer in chan_peers:
+        pl.semaphore_signal(barrier, inc=1, device_id={"chan": peer}, device_id_type=MESH)
+    for peer in row_peers:
+        pl.semaphore_signal(barrier, inc=1, device_id={"rows": peer}, device_id_type=MESH)
+
     loads = [
         pltpu.make_async_copy(src, dst, load_sem.at[k])
         for k, (src, dst) in enumerate(
@@ -186,16 +226,31 @@
             )
         )
     ]
-    for load in loads:
+    smalls = [
+        pltpu.make_async_copy(src, dst, small_sem.at[k])
+        for k, (src, dst) in enumerate(
+            (
+                (shift_mid_h, shift_mid),
+                (gain_mid_h, gain_mid),
+                (lower_mid_h, lower_mid),
+                (upper_mid_h, upper_mid),
+                (diag_mid_h, diag_mid),
+                (first_bias_mid_h, first_bias_mid),
+                (second_bias_mid_h, second_bias_mid),
+                (third_bias_mid_h, third_bias_mid),
+                (shift_top_h, shift_top),
+                (gain_top_h, gain_top),
+                (lower_top_h, lower_top),
+                (upper_top_h, upper_top),
+                (diag_top_h, diag_top),
+                (first_bias_top_h, first_bias_top),
+                (second_bias_top_h, second_bias_top),
+                (third_bias_top_h, third_bias_top),
+            )
+        )
+    ]
+    for load in (loads[0], *smalls, *loads[1:]):
         load.start()
-
-    barrier = pltpu.get_barrier_semaphore()
-    chan_peers = [lax.rem(me_chan + k, n_chan) for k in range(1, n_chan)]
-    row_peers = [lax.rem(me_row + k, n_rows) for k in range(1, n_rows)]
-    for peer in chan_peers:
-        pl.semaphore_signal(barrier, inc=1, device_id={"chan": peer}, device_id_type=MESH)
-    for peer in row_peers:
-        pl.semaphore_signal(barrier, inc=1, device_id={"rows": peer}, device_id_type=MESH)
 
     loads[0].wait()
     for i in range(n_img):
@@ -205,6 +260,22 @@
         y_out[i] = jnp.concatenate(packed, axis=1)
     y_in[me_chan] = y_out[me_chan]
 
+    pl.semaphore_wait(barrier, n_chan + n_rows - 2)
+    y_copies = []
+    for k, peer in enumerate(chan_peers):
+        copy = pltpu.make_async_remote_copy(
+            src_ref=y_out.at[peer],
+            dst_ref=y_in.at[me_chan],
+            send_sem=ys_sem.at[k],
+            recv_sem=yr_sem.at[n_chan - 2 - k],
+            device_id={"chan": peer},
+            device_id_type=MESH,
+        )
+        copy.start()
+        y_copies.append(copy)
+
+    for load in smalls:
+        load.wait()
     spread = jnp.where(
         iota2((32, c_mid), 0)
         == iota2((32, c_mid), 1) + jnp.where(iota2((32, c_mid), 1) >= half_m, 16 - half_m, 0),
@@ -250,20 +321,6 @@
             mix_p1[s - 1] = mix
         const_p[s] = const
 
-    pl.semaphore_wait(barrier, n_chan + n_rows - 2)
-    y_copies = []
-    for k, peer in enumerate(chan_peers):
-        copy = pltpu.make_async_remote_copy(
-            src_ref=y_out.at[peer],
-            dst_ref=y_in.at[me_chan],
-            send_sem=ys_sem.at[k],
-            recv_sem=yr_sem.at[n_chan - 2 - k],
-            device_id={"chan": peer},
-            device_id_type=MESH,
-        )
-        copy.start()
-        y_copies.append(copy)
-
     def prepare_mid(s):
         w1f_m[...] = jnp.zeros_like(w1f_m)
         for t in range(9):
@@ -281,9 +338,14 @@
         w2p_t[s] = w2p[s].T
         b2p[s] = jnp.broadcast_to(second_bias_top[s : s + 1], (128, b2p.shape[1])).T
 
-    loads[1].wait()
-    loads[2].wait()
-    prepare_mid(0)
+    for load in loads[1:]:
+        load.wait()
+    for s in range(steps_m):
+        prepare_mid(s)
+    for s in range(steps_p):
+        prepare_top(s)
+    bias3_m = [column(third_bias_mid[s : s + 1]) for s in range(steps_m)]
+    bias3_p = [column(third_bias_top[s : s + 1]) for s in range(steps_p)]
 
     for copy in y_copies:
         copy.wait_recv()
@@ -304,14 +366,6 @@
         )
         copy.start()
         z_copies.append(copy)
-    for s in range(1, steps_m):
-        prepare_mid(s)
-    for load in loads[3:]:
-        load.wait()
-    for s in range(steps_p):
-        prepare_top(s)
-    bias3_m = [column(third_bias_mid[s : s + 1]) for s in range(steps_m)]
-    bias3_p = [column(third_bias_top[s : s + 1]) for s in range(steps_p)]
     for copy in z_copies:
         copy.wait_recv()
     state = jnp.concatenate([z_in[2].astype(F32), z_in[0].astype(F32), own, z_in[1].astype(F32), z_in[3].astype(F32)], axis=1)
@@ -354,7 +408,7 @@
             row >= 1,
             row <= height - 2,
             width,
-            256,
+            512,
             False,
         )
         state = jnp.concatenate([ua, updated], axis=0)
@@ -443,8 +497,8 @@
         copy.wait_recv()
     for c in range(n_img):
         piece = back_in[c]
-        latent_mid[c, :8] = piece[:, :width]
-        latent_mid[c, 8:half_m] = piece[: half_m - 8, width : 2 * width]
+        latent_mid[half_m * c : half_m * c + 8] = piece[:, :width]
+        latent_mid[half_m * c + 8 : half_m * (c + 1)] = piece[: half_m - 8, width : 2 * width]
     cells = height * width
     const = sum(
         (
@@ -461,6 +515,15 @@
     loglik[...] = jnp.broadcast_to((jnp.sum(total) + const) * scale - 0.5 * log_two_pi, (1, 128))
     for copy in (*y_copies, *z_copies, *back_copies, *ll_copies):
         copy.wait_send()
+
+
+def write_out(*refs):
+    sem = refs[-1]
+    copies = [pltpu.make_async_copy(refs[k], refs[3 + k], sem.at[k]) for k in range(3)]
+    for copy in copies:
+        copy.start()
+    for copy in copies:
+        copy.wait()
 
 
 def body(
@@ -498,20 +561,20 @@
     third_mid = third_mid.transpose(0, 1, 3, 2).reshape(steps_m, 9 * c_mid, hid)
     third_top = third_top.transpose(0, 1, 3, 2).reshape(steps_p, 9 * c_top, hid)
     first_top = first_top.reshape(steps_p, 9 * half_p, hid)
-    big = pl.BlockSpec(memory_space=pl.ANY)
+    big = pl.BlockSpec(memory_space=pltpu.HBM)
     small = pl.BlockSpec(memory_space=pltpu.VMEM)
-    where = [big] + [small] * 5 + [big, small] * 2 + [big, small] + [small] * 5 + [big, small] * 3
     rows_p = n_chan // 2
     vmem = pltpu.VMEM
+    small_args = (shift_mid, gain_mid, lower_mid, upper_mid, diag_mid, first_bias_mid, second_bias_mid, third_bias_mid, shift_top, gain_top, lower_top, upper_top, diag_top, first_bias_top, second_bias_top, third_bias_top)
     dma = pltpu.SemaphoreType.DMA
-    latent_mid, latent_top, loglik = pl.pallas_call(
+    found = pl.pallas_call(
         functools.partial(kernel, n_rows, n_chan),
         out_shape=(
-            jax.ShapeDtypeStruct((n_img, half_m, width), F32),
-            jax.ShapeDtypeStruct((rows_p * width // 2, c_top), F32),
-            jax.ShapeDtypeStruct((1, 128), F32),
+            vmem((n_img * half_m, width), F32),
+            vmem((rows_p * width // 2, c_top), F32),
+            vmem((1, 128), F32),
         ),
-        in_specs=where,
+        in_specs=[big] * 23,
         out_specs=(small, small, small),
         scratch_shapes=[
             vmem((n_img, c_mid, width), F32),
@@ -542,7 +605,9 @@
             vmem((n_chan, 8, 128), F32),
             vmem((1, 128), F32),
             vmem((n_rows - 1, 1, 128), F32),
+            *(vmem(a.shape, a.dtype) for a in small_args),
             dma((7,)),
+            dma((len(small_args),)),
             dma((n_chan - 1,)),
             dma((n_chan - 1,)),
             dma((4,)),
@@ -553,7 +618,7 @@
             dma((n_rows - 1,)),
         ],
         compiler_params=pltpu.CompilerParams(
-            collective_id=0, has_side_effects=True, vmem_limit_bytes=66 * 1000 * 1000
+            collective_id=0, has_side_effects=True, vmem_limit_bytes=67043328 - 100 * 1024
         ),
     )(
         images,
@@ -580,6 +645,14 @@
         third_top,
         third_bias_top,
     )
+    latent_mid, latent_top, loglik = pl.pallas_call(
+        write_out,
+        out_shape=tuple(jax.ShapeDtypeStruct(x.shape, x.dtype) for x in found),
+        in_specs=[small] * 3,
+        out_specs=(pl.BlockSpec(memory_space=pltpu.HBM),) * 3,
+        scratch_shapes=[dma((3,))],
+        compiler_params=pltpu.CompilerParams(vmem_limit_bytes=1024 * 1024),
+    )(*found)
     latent_mid = latent_mid.reshape(n_img, half_m, 1, width)
     latent_top = latent_top.reshape(1, rows_p, width // 2, c_top).transpose(0, 3, 1, 2)
     return latent_mid, latent_top, loglik[0, :1]

time: 47.8 us -> 38.4 us (0.80)
  Pallas kernels: 42.2 us -> 37.6 us
  local copies, waits for them, and re-layouts: 2.88 us -> 0 us
  between operations: 2.47 us -> 0.65 us
    pallas_call x1 -> x2, Pallas kernels: 42.2 us -> 37.6 us  [the longest x1 36.9 us: body(): pl.pallas_call(functools.partial(kernel, n_rows, n_chan), out_shape=(vmem...]
    unnamed x2 -> x0, local copies, waits for them, and re-layouts: 2.88 us -> none
where the time goes in v2:
time: 38.4 us; the launch traced here: 38.2 us
  Pallas kernels  37.6 us (98%)
  between operations  0.65 us (2%)
    pallas_call x1, Pallas kernels, body(): pl.pallas_call(functools.partial(kernel, n_rows, n_chan), out_shape=(vmem...  36.9 us

profile of v2, /device:TPU:6, one launch (start us, length us, event | category | flops | bytes accessed | tf_op | source)
XLA Modules:
  0.0 38.2 jit_solution(940707861025026507)
XLA Ops:
  0.6 36.9 %shard_map.238 = (f32[96,32]{1,0:T(8,128)S(1)}, f32[64,48]{1,0:T(8,128)S(1)}, f32[1,128]{1,0:T(1,128)S(1)}) custom-call(f32[8,24,32]{2,1,0:T(8,128)} %bitcast.17, f32[3,24]{1,0:T(4,128)} %shift_mid_h.1, f32[3,24]{1,0:T(4,128)} %gain_mid_h.1, f32[3,24,24]{2,1,0:T(8,128)} %lower_mid_h.1, f32[3,24,24]{2,1,0:T(8,128)} %upper_mid_h.1, f32[3,24]{1,0:T(4,128)} %diag_mid_h.1, ...), custom_call_target="tpu_custom_call" | custom-call | tf_op jit(solution)/shard_map/pallas_call | solution.py:570
  37.6 0.7 %shard_map.239 = (f32[96,32]{1,0:T(8,128)}, f32[64,48]{1,0:T(8,128)}, f32[1,128]{1,0:T(1,128)}) custom-call(f32[96,32]{1,0:T(8,128)S(1)} %get-tuple-element.9.refs_0_, f32[64,48]{1,0:T(8,128)S(1)} %get-tuple-element.10.refs_1_, f32[1,128]{1,0:T(1,128)S(1)} %get-tuple-element.11.refs_2_), custom_call_target="tpu_custom_call" | custom-call | tf_op jit(solution)/shard_map/pallas_call | solution.py:648

commit v3 on v2

--- a/solution.py
+++ b/solution.py
@@ -61,17 +61,26 @@
     )
 
 
-def coupling(u, half, pad, w1t, w2t, bias2, w3, bias3, left_ok, right_ok, up_ok, down_ok, cols, tile, extra):
+def shifted(x, by, ok):
+    pieces = [pltpu.roll(x[:, at : at + 128], by, 1) for at in range(0, x.shape[1], 128)]
+    return jnp.where(ok, jnp.concatenate(pieces, axis=1), 0.0)
+
+
+def from_left(x, ok):
+    return shifted(x, 1, ok)
+
+
+def from_right(x, ok):
+    return shifted(x, 127, ok)
+
+
+def coupling(u, half, pad, w1t, w2t, bias2, w3, bias3, left_ok, right_ok, up_ok, down_ok, inside, cols, tile, extra):
     length = u.shape[1]
     ua, ub = u[:pad], u[pad : 2 * pad]
-    q = ua.astype(BF16).astype(F32)
-    sides = (
-        jnp.where(left_ok, pltpu.roll(q, 1, 1), 0.0),
-        q,
-        jnp.where(right_ok, pltpu.roll(q, length - 1, 1), 0.0),
-    )
-    above = [jnp.where(up_ok, pltpu.roll(s, cols, 1), 0.0) for s in sides]
-    below = [jnp.where(down_ok, pltpu.roll(s, length - cols, 1), 0.0) for s in sides]
+    q = jnp.where(inside, ua.astype(BF16).astype(F32), 0.0)
+    sides = (from_left(q, left_ok), q, from_right(q, right_ok))
+    above = [pltpu.roll(s, cols, 1) for s in sides]
+    below = [pltpu.roll(s, length - cols, 1) for s in sides]
     stack = [*above, *sides, *below]
     if extra:
         stack.append(jnp.ones((8, length), F32))
@@ -93,8 +102,8 @@
         a, b, c = (taps[(dr * 3 + dc) * both : (dr * 3 + dc + 1) * both] for dc in range(3))
         rows.append(
             b
-            + jnp.where(left_ok, pltpu.roll(a, 1, 1), 0.0)
-            + jnp.where(right_ok, pltpu.roll(c, length - 1, 1), 0.0)
+            + from_left(a, left_ok)
+            + from_right(c, right_ok)
         )
     out = (
         rows[1]
@@ -166,6 +175,8 @@
     y_in,
     z_out,
     z_in,
+    k_out,
+    k_in,
     back_out,
     back_in,
     ll_out,
@@ -187,11 +198,14 @@
     second_bias_top,
     third_bias_top,
     load_sem,
+    image_sem,
     small_sem,
     ys_sem,
     yr_sem,
     zs_sem,
     zr_sem,
+    ks_sem,
+    kr_sem,
     bs_sem,
     br_sem,
     ls_sem,
@@ -204,19 +218,22 @@
     c_top = shift_top.shape[1]
     half_p = c_top // 2
 
+    image_load = pltpu.make_async_copy(images, img_v, image_sem)
+    image_load.start()
     barrier = pltpu.get_barrier_semaphore()
+    far = sorted(range(1, n_chan), key=lambda k: -min(k, n_chan - k))
     chan_peers = [lax.rem(me_chan + k, n_chan) for k in range(1, n_chan)]
     row_peers = [lax.rem(me_row + k, n_rows) for k in range(1, n_rows)]
-    for peer in chan_peers:
-        pl.semaphore_signal(barrier, inc=1, device_id={"chan": peer}, device_id_type=MESH)
-    for peer in row_peers:
-        pl.semaphore_signal(barrier, inc=1, device_id={"rows": peer}, device_id_type=MESH)
+    near = sorted({d % n_rows for d in (1, -1, 2, -2)} - {0})
+    for k in far:
+        pl.semaphore_signal(barrier, inc=1, device_id={"chan": chan_peers[k - 1]}, device_id_type=MESH)
+    for d in near:
+        pl.semaphore_signal(barrier, inc=1, device_id={"rows": row_peers[d - 1]}, device_id_type=MESH)
 
     loads = [
         pltpu.make_async_copy(src, dst, load_sem.at[k])
         for k, (src, dst) in enumerate(
             (
-                (images, img_v),
                 (first_mid, w1m),
                 (second_mid, w2m),
                 (third_mid, w3m),
@@ -249,10 +266,10 @@
             )
         )
     ]
-    for load in (loads[0], *smalls, *loads[1:]):
+    for load in (*smalls, *loads):
         load.start()
 
-    loads[0].wait()
+    image_load.wait()
     for i in range(n_img):
         row = img_v[i]
         packed = [row[8 * k : 8 * k + 8] for k in range(c_mid // 8)]
@@ -260,7 +277,7 @@
         y_out[i] = jnp.concatenate(packed, axis=1)
     y_in[me_chan] = y_out[me_chan]
 
-    pl.semaphore_wait(barrier, n_chan + n_rows - 2)
+    pl.semaphore_wait(barrier, n_chan - 1 + len(near))
     y_copies = []
     for k, peer in enumerate(chan_peers):
         copy = pltpu.make_async_remote_copy(
@@ -338,7 +355,7 @@
         w2p_t[s] = w2p[s].T
         b2p[s] = jnp.broadcast_to(second_bias_top[s : s + 1], (128, b2p.shape[1])).T
 
-    for load in loads[1:]:
+    for load in loads:
         load.wait()
     for s in range(steps_m):
         prepare_mid(s)
@@ -355,7 +372,7 @@
     own = jnp.concatenate([*groups, jnp.zeros((32 - c_mid, n_chan * width), F32)], axis=0)
     z_out[...] = own.astype(BF16)
     z_copies = []
-    for k, d in enumerate((1, -1, 2, -2)):
+    for k, d in enumerate((1, -1)):
         copy = pltpu.make_async_remote_copy(
             src_ref=z_out,
             dst_ref=z_in.at[k],
@@ -368,7 +385,7 @@
         z_copies.append(copy)
     for copy in z_copies:
         copy.wait_recv()
-    state = jnp.concatenate([z_in[2].astype(F32), z_in[0].astype(F32), own, z_in[1].astype(F32), z_in[3].astype(F32)], axis=1)
+    state = jnp.concatenate([z_in[0].astype(F32), own, z_in[1].astype(F32)], axis=1)
 
     height = n_rows * n_chan
     partial = jnp.zeros((8, 128), F32)
@@ -381,13 +398,13 @@
                 total = piece if total is None else total + piece
         return total
 
-    first_row = me_row * n_chan - 2 * n_chan
-    own_at = 2 * n_chan * width
+    first_row = me_row * n_chan - n_chan
+    own_at = n_chan * width
     own_lanes = n_chan * width
     valid_m = iota2((16, own_lanes), 0) < half_m
     for s in range(steps_m):
         if s == 1:
-            state = state[:, 4 * width : 36 * width]
+            state = state[:, 4 * width : 20 * width]
             first_row = first_row + 4
             own_at = own_at - 4 * width
         length = state.shape[1]
@@ -407,6 +424,7 @@
             col <= width - 2,
             row >= 1,
             row <= height - 2,
+            jnp.logical_and(row >= 0, row < height),
             width,
             512,
             False,
@@ -414,6 +432,20 @@
         state = jnp.concatenate([ua, updated], axis=0)
         mine = g[:, own_at : own_at + own_lanes]
         partial = partial + folded(jnp.where(valid_m, log_sigmoid(mine), 0.0))
+    kept = state[16:, own_at : own_at + own_lanes]
+    k_out[...] = kept.astype(BF16)
+    k_copies = []
+    for k, d in enumerate((1, -1)):
+        copy = pltpu.make_async_remote_copy(
+            src_ref=k_out,
+            dst_ref=k_in.at[k],
+            send_sem=ks_sem.at[k],
+            recv_sem=kr_sem.at[k],
+            device_id={"rows": lax.rem(me_row + d + n_rows, n_rows)},
+            device_id_type=MESH,
+        )
+        copy.start()
+        k_copies.append(copy)
     latent = jnp.where(valid_m, state[:16, own_at : own_at + own_lanes], 0.0)
     partial = partial + folded(-0.5 * latent * latent)
 
@@ -434,11 +466,13 @@
         copy.start()
         back_copies.append(copy)
 
-    kept = state[16:, 4 * width : 28 * width]
     cols_p = width // 2
     lane = iota2((16, 128), 1)
     phase, rest = lax.div(lane, 32), lax.rem(lane, 32)
     pick = (2 * lax.div(rest, cols_p) + lax.div(phase, 2)) * width + 2 * lax.rem(rest, cols_p) + lax.rem(phase, 2)
+    for copy in k_copies:
+        copy.wait_recv()
+    kept = jnp.concatenate([k_in[0].astype(F32), kept, k_in[1].astype(F32)], axis=1)
     blocks = [
         jnp.take_along_axis(kept[:, 128 * k : 128 * k + 128], pick, axis=1) for k in range(kept.shape[1] // 128)
     ]
@@ -471,6 +505,7 @@
             col <= cols_p - 2,
             row >= 1,
             row <= height // 2 - 2,
+            jnp.logical_and(row >= 0, row < height // 2),
             cols_p,
             256,
             True,
@@ -513,7 +548,7 @@
         total = total + ll_in[k]
     scale = 1.0 / (c_mid * cells)
     loglik[...] = jnp.broadcast_to((jnp.sum(total) + const) * scale - 0.5 * log_two_pi, (1, 128))
-    for copy in (*y_copies, *z_copies, *back_copies, *ll_copies):
+    for copy in (*y_copies, *z_copies, *k_copies, *back_copies, *ll_copies):
         copy.wait_send()
 
 
@@ -600,18 +635,23 @@
             vmem((n_chan, 8, 128), F32),
             vmem((n_chan, 8, 128), F32),
             vmem((32, n_chan * width), BF16),
-            vmem((4, 32, n_chan * width), BF16),
+            vmem((2, 32, n_chan * width), BF16),
+            vmem((16, n_chan * width), BF16),
+            vmem((2, 16, n_chan * width), BF16),
             vmem((n_chan, 8, 128), F32),
             vmem((n_chan, 8, 128), F32),
             vmem((1, 128), F32),
             vmem((n_rows - 1, 1, 128), F32),
             *(vmem(a.shape, a.dtype) for a in small_args),
-            dma((7,)),
+            dma((6,)),
+            dma(()),
             dma((len(small_args),)),
             dma((n_chan - 1,)),
             dma((n_chan - 1,)),
-            dma((4,)),
-            dma((4,)),
+            dma((2,)),
+            dma((2,)),
+            dma((2,)),
+            dma((2,)),
             dma((n_chan - 1,)),
             dma((n_chan - 1,)),
             dma((n_rows - 1,)),

time: 38.4 us -> 37.2 us (0.969)
  Pallas kernels: 37.6 us -> 36.5 us
    pallas_call x1, Pallas kernels: 36.9 us -> 35.8 us  [body(): pl.pallas_call(functools.partial(kernel, n_rows, n_chan), out_shape=(vmem...]
where the time goes in v3:
time: 37.2 us; the launch traced here: 37.1 us
  Pallas kernels  36.5 us (98%)
  between operations  0.65 us (2%)
    pallas_call x1, Pallas kernels, body(): pl.pallas_call(functools.partial(kernel, n_rows, n_chan), out_shape=(vmem...  35.8 us

profile of v3, /device:TPU:6, one launch (start us, length us, event | category | flops | bytes accessed | tf_op | source)
XLA Modules:
  0.0 37.1 jit_solution(3789885351833171189)
XLA Ops:
  0.6 35.8 %shard_map.238 = (f32[96,32]{1,0:T(8,128)S(1)}, f32[64,48]{1,0:T(8,128)S(1)}, f32[1,128]{1,0:T(1,128)S(1)}) custom-call(f32[8,24,32]{2,1,0:T(8,128)} %bitcast.17, f32[3,24]{1,0:T(4,128)} %shift_mid_h.1, f32[3,24]{1,0:T(4,128)} %gain_mid_h.1, f32[3,24,24]{2,1,0:T(8,128)} %lower_mid_h.1, f32[3,24,24]{2,1,0:T(8,128)} %upper_mid_h.1, f32[3,24]{1,0:T(4,128)} %diag_mid_h.1, ...), custom_call_target="tpu_custom_call" | custom-call | tf_op jit(solution)/shard_map/pallas_call | solution.py:605
  36.4 0.7 %shard_map.239 = (f32[96,32]{1,0:T(8,128)}, f32[64,48]{1,0:T(8,128)}, f32[1,128]{1,0:T(1,128)}) custom-call(f32[96,32]{1,0:T(8,128)S(1)} %get-tuple-element.9.refs_0_, f32[64,48]{1,0:T(8,128)S(1)} %get-tuple-element.10.refs_1_, f32[1,128]{1,0:T(1,128)S(1)} %get-tuple-element.11.refs_2_), custom_call_target="tpu_custom_call" | custom-call | tf_op jit(solution)/shard_map/pallas_call | solution.py:688

commit v4 on v3

--- a/solution.py
+++ b/solution.py
@@ -210,6 +210,7 @@
     br_sem,
     ls_sem,
     lr_sem,
+    token_sem,
 ):
     me_row, me_chan = lax.axis_index("rows"), lax.axis_index("chan")
     steps_m, steps_p = shift_mid.shape[0], shift_top.shape[0]
@@ -218,17 +219,47 @@
     c_top = shift_top.shape[1]
     half_p = c_top // 2
 
+    def has_row(d):
+        return jnp.logical_and(me_row + d >= 0, me_row + d < n_rows)
+
+    def to_neighbours(src, dst, send_sem, recv_sem):
+        copies = []
+        for k, d in enumerate((1, -1)):
+            copy = pltpu.make_async_remote_copy(
+                src_ref=src,
+                dst_ref=dst.at[k],
+                send_sem=send_sem.at[k],
+                recv_sem=recv_sem.at[k],
+                device_id={"rows": lax.rem(me_row + d + n_rows, n_rows)},
+                device_id_type=MESH,
+            )
+            pl.when(has_row(d))(copy.start)
+            copies.append((copy, d))
+        return copies
+
+    def from_neighbours(copies):
+        for copy, d in copies:
+            pl.when(has_row(-d))(copy.wait_recv)
+
+    def tell_rows(sem, by):
+        for d in (by, -by):
+
+            @pl.when(has_row(d))
+            def _():
+                pl.semaphore_signal(sem, inc=1, device_id={"rows": lax.rem(me_row + d + n_rows, n_rows)}, device_id_type=MESH)
+
+    def rows_off(by):
+        return has_row(by).astype(jnp.int32) + has_row(-by).astype(jnp.int32)
+
     image_load = pltpu.make_async_copy(images, img_v, image_sem)
     image_load.start()
     barrier = pltpu.get_barrier_semaphore()
     far = sorted(range(1, n_chan), key=lambda k: -min(k, n_chan - k))
     chan_peers = [lax.rem(me_chan + k, n_chan) for k in range(1, n_chan)]
     row_peers = [lax.rem(me_row + k, n_rows) for k in range(1, n_rows)]
-    near = sorted({d % n_rows for d in (1, -1, 2, -2)} - {0})
     for k in far:
         pl.semaphore_signal(barrier, inc=1, device_id={"chan": chan_peers[k - 1]}, device_id_type=MESH)
-    for d in near:
-        pl.semaphore_signal(barrier, inc=1, device_id={"rows": row_peers[d - 1]}, device_id_type=MESH)
+    tell_rows(barrier, 1)
 
     loads = [
         pltpu.make_async_copy(src, dst, load_sem.at[k])
@@ -277,7 +308,8 @@
         y_out[i] = jnp.concatenate(packed, axis=1)
     y_in[me_chan] = y_out[me_chan]
 
-    pl.semaphore_wait(barrier, n_chan - 1 + len(near))
+    pl.semaphore_wait(barrier, n_chan - 1 + rows_off(1))
+    tell_rows(token_sem.at[0], 1)
     y_copies = []
     for k, peer in enumerate(chan_peers):
         copy = pltpu.make_async_remote_copy(
@@ -371,21 +403,19 @@
         groups.append(jnp.concatenate([y_in[c][:, width * k : width * (k + 1)] for c in range(n_chan)], axis=1))
     own = jnp.concatenate([*groups, jnp.zeros((32 - c_mid, n_chan * width), F32)], axis=0)
     z_out[...] = own.astype(BF16)
-    z_copies = []
-    for k, d in enumerate((1, -1)):
-        copy = pltpu.make_async_remote_copy(
-            src_ref=z_out,
-            dst_ref=z_in.at[k],
-            send_sem=zs_sem.at[k],
-            recv_sem=zr_sem.at[k],
-            device_id={"rows": lax.rem(me_row + d + n_rows, n_rows)},
-            device_id_type=MESH,
-        )
-        copy.start()
-        z_copies.append(copy)
-    for copy in z_copies:
-        copy.wait_recv()
-    state = jnp.concatenate([z_in[0].astype(F32), own, z_in[1].astype(F32)], axis=1)
+    z_copies = to_neighbours(z_out, z_in, zs_sem, zr_sem)
+    pl.semaphore_wait(token_sem.at[0], rows_off(1))
+    tell_rows(token_sem.at[1], 2)
+    from_neighbours(z_copies)
+    zero = jnp.zeros_like(own)
+    state = jnp.concatenate(
+        [
+            jnp.where(has_row(-1), z_in[0].astype(F32), zero),
+            own,
+            jnp.where(has_row(1), z_in[1].astype(F32), zero),
+        ],
+        axis=1,
+    )
 
     height = n_rows * n_chan
     partial = jnp.zeros((8, 128), F32)
@@ -434,18 +464,7 @@
         partial = partial + folded(jnp.where(valid_m, log_sigmoid(mine), 0.0))
     kept = state[16:, own_at : own_at + own_lanes]
     k_out[...] = kept.astype(BF16)
-    k_copies = []
-    for k, d in enumerate((1, -1)):
-        copy = pltpu.make_async_remote_copy(
-            src_ref=k_out,
-            dst_ref=k_in.at[k],
-            send_sem=ks_sem.at[k],
-            recv_sem=kr_sem.at[k],
-            device_id={"rows": lax.rem(me_row + d + n_rows, n_rows)},
-            device_id_type=MESH,
-        )
-        copy.start()
-        k_copies.append(copy)
+    k_copies = to_neighbours(k_out, k_in, ks_sem, kr_sem)
     latent = jnp.where(valid_m, state[:16, own_at : own_at + own_lanes], 0.0)
     partial = partial + folded(-0.5 * latent * latent)
 
@@ -470,9 +489,18 @@
     lane = iota2((16, 128), 1)
     phase, rest = lax.div(lane, 32), lax.rem(lane, 32)
     pick = (2 * lax.div(rest, cols_p) + lax.div(phase, 2)) * width + 2 * lax.rem(rest, cols_p) + lax.rem(phase, 2)
-    for copy in k_copies:
-        copy.wait_recv()
-    kept = jnp.concatenate([k_in[0].astype(F32), kept, k_in[1].astype(F32)], axis=1)
+    pl.semaphore_wait(token_sem.at[1], rows_off(2))
+    tell_rows(token_sem.at[2], 4)
+    from_neighbours(k_copies)
+    zero = jnp.zeros_like(kept)
+    kept = jnp.concatenate(
+        [
+            jnp.where(has_row(-1), k_in[0].astype(F32), zero),
+            kept,
+            jnp.where(has_row(1), k_in[1].astype(F32), zero),
+        ],
+        axis=1,
+    )
     blocks = [
         jnp.take_along_axis(kept[:, 128 * k : 128 * k + 128], pick, axis=1) for k in range(kept.shape[1] // 128)
     ]
@@ -485,12 +513,14 @@
 
     rows_p = n_chan // 2
     first_row = me_row * rows_p - rows_p
-    length = state.shape[1]
-    lane = iota2((1, length), 1)
-    col, row = lax.rem(lane, cols_p), lax.div(lane, cols_p) + first_row
     own_at = rows_p * cols_p
-    mine_p = jnp.logical_and(lane >= own_at, lane < 2 * own_at)
     for s in range(steps_p):
+        if s == steps_p - 1:
+            state = pltpu.roll(state, state.shape[1] - 2 * cols_p, 1)[:, :128]
+            first_row, own_at = first_row + 2, own_at - 2 * cols_p
+        lane = iota2((1, state.shape[1]), 1)
+        col, row = lax.rem(lane, cols_p), lax.div(lane, cols_p) + first_row
+        mine_p = jnp.logical_and(lane >= own_at, lane < own_at + rows_p * cols_p)
         u = apply_mix(state, mix_p0[...] if s == 0 else mix_p1[s - 1], const_p[s])
         ua, updated, g = coupling(
             u,
@@ -514,6 +544,7 @@
         partial = partial + folded(jnp.where(mine_p, log_sigmoid(g), 0.0))
     partial = partial + folded(jnp.where(mine_p, -0.5 * state * state, 0.0))
     ll_out[...] = jnp.sum(partial, axis=0, keepdims=True)
+    pl.semaphore_wait(token_sem.at[2], rows_off(4))
     ll_copies = []
     for k, peer in enumerate(row_peers):
         copy = pltpu.make_async_remote_copy(
@@ -527,7 +558,7 @@
         copy.start()
         ll_copies.append(copy)
 
-    latent_top[...] = state[:, :128].T[own_at : 2 * own_at]
+    latent_top[...] = state.T[own_at : own_at + rows_p * cols_p]
     for copy in back_copies:
         copy.wait_recv()
     for c in range(n_img):
@@ -548,8 +579,11 @@
         total = total + ll_in[k]
     scale = 1.0 / (c_mid * cells)
     loglik[...] = jnp.broadcast_to((jnp.sum(total) + const) * scale - 0.5 * log_two_pi, (1, 128))
-    for copy in (*y_copies, *z_copies, *k_copies, *back_copies, *ll_copies):
+    for copy in (*y_copies, *back_copies, *ll_copies):
         copy.wait_send()
+    for copies in (z_copies, k_copies):
+        for copy, d in copies:
+            pl.when(has_row(d))(copy.wait_send)
 
 
 def write_out(*refs):
@@ -656,6 +690,7 @@
             dma((n_chan - 1,)),
             dma((n_rows - 1,)),
             dma((n_rows - 1,)),
+            pltpu.SemaphoreType.REGULAR((3,)),
         ],
         compiler_params=pltpu.CompilerParams(
             collective_id=0, has_side_effects=True, vmem_limit_bytes=67043328 - 100 * 1024

time: 37.2 us -> 36.2 us (0.973)
  Pallas kernels: 36.5 us -> 35.4 us
    pallas_call x1, Pallas kernels: 35.8 us -> 34.8 us  [body(): pl.pallas_call(functools.partial(kernel, n_rows, n_chan), out_shape=(vmem...]
where the time goes in v4:
time: 36.2 us; the launch traced here: 36.1 us
  Pallas kernels  35.4 us (98%)
  between operations  0.65 us (2%)
    pallas_call x1, Pallas kernels, body(): pl.pallas_call(functools.partial(kernel, n_rows, n_chan), out_shape=(vmem...  34.8 us

profile of v4, /device:TPU:6, one launch (start us, length us, event | category | flops | bytes accessed | tf_op | source)
XLA Modules:
  0.0 36.1 jit_solution(9731395624995311817)
XLA Ops:
  0.6 34.8 %shard_map.238 = (f32[96,32]{1,0:T(8,128)S(1)}, f32[64,48]{1,0:T(8,128)S(1)}, f32[1,128]{1,0:T(1,128)S(1)}) custom-call(f32[8,24,32]{2,1,0:T(8,128)} %bitcast.17, f32[3,24]{1,0:T(4,128)} %shift_mid_h.1, f32[3,24]{1,0:T(4,128)} %gain_mid_h.1, f32[3,24,24]{2,1,0:T(8,128)} %lower_mid_h.1, f32[3,24,24]{2,1,0:T(8,128)} %upper_mid_h.1, f32[3,24]{1,0:T(4,128)} %diag_mid_h.1, ...), custom_call_target="tpu_custom_call" | custom-call | tf_op jit(solution)/shard_map/pallas_call | solution.py:639
  35.4 0.7 %shard_map.239 = (f32[96,32]{1,0:T(8,128)}, f32[64,48]{1,0:T(8,128)}, f32[1,128]{1,0:T(1,128)}) custom-call(f32[96,32]{1,0:T(8,128)S(1)} %get-tuple-element.9.refs_0_, f32[64,48]{1,0:T(8,128)S(1)} %get-tuple-element.10.refs_1_, f32[1,128]{1,0:T(1,128)S(1)} %get-tuple-element.11.refs_2_), custom_call_target="tpu_custom_call" | custom-call | tf_op jit(solution)/shard_map/pallas_call | solution.py:723

commit v5 on v4

--- a/solution.py
+++ b/solution.py
@@ -173,7 +173,6 @@
     const_p,
     y_out,
     y_in,
-    z_out,
     z_in,
     k_out,
     k_in,
@@ -215,6 +214,7 @@
     me_row, me_chan = lax.axis_index("rows"), lax.axis_index("chan")
     steps_m, steps_p = shift_mid.shape[0], shift_top.shape[0]
     n_img, c_mid, width = img_v.shape
+    halo = 2 * steps_m
     half_m = c_mid // 2
     c_top = shift_top.shape[1]
     half_p = c_top // 2
@@ -254,9 +254,10 @@
     image_load = pltpu.make_async_copy(images, img_v, image_sem)
     image_load.start()
     barrier = pltpu.get_barrier_semaphore()
-    far = sorted(range(1, n_chan), key=lambda k: -min(k, n_chan - k))
-    chan_peers = [lax.rem(me_chan + k, n_chan) for k in range(1, n_chan)]
+    far = sorted(range(1, n_chan), key=lambda k: (-(k // 2 == 2), -(k > 1)))
+    chan_peers = [me_chan ^ k for k in range(1, n_chan)]
     row_peers = [lax.rem(me_row + k, n_rows) for k in range(1, n_rows)]
+    far_rows = sorted(range(1, n_rows), key=lambda k: -min(k, n_rows - k))
     for k in far:
         pl.semaphore_signal(barrier, inc=1, device_id={"chan": chan_peers[k - 1]}, device_id_type=MESH)
     tell_rows(barrier, 1)
@@ -311,12 +312,13 @@
     pl.semaphore_wait(barrier, n_chan - 1 + rows_off(1))
     tell_rows(token_sem.at[0], 1)
     y_copies = []
-    for k, peer in enumerate(chan_peers):
+    for k in far:
+        peer = chan_peers[k - 1]
         copy = pltpu.make_async_remote_copy(
             src_ref=y_out.at[peer],
             dst_ref=y_in.at[me_chan],
-            send_sem=ys_sem.at[k],
-            recv_sem=yr_sem.at[n_chan - 2 - k],
+            send_sem=ys_sem.at[k - 1],
+            recv_sem=yr_sem.at[k - 1],
             device_id={"chan": peer},
             device_id_type=MESH,
         )
@@ -396,23 +398,57 @@
     bias3_m = [column(third_bias_mid[s : s + 1]) for s in range(steps_m)]
     bias3_p = [column(third_bias_top[s : s + 1]) for s in range(steps_p)]
 
-    for copy in y_copies:
+    z_copies = []
+
+    def forward(c):
+        for k, (d, needed) in enumerate(((1, c >= n_chan - halo), (-1, c < halo))):
+            copy = pltpu.make_async_remote_copy(
+                src_ref=y_in.at[c],
+                dst_ref=z_in.at[k, c],
+                send_sem=zs_sem.at[k, c],
+                recv_sem=zr_sem.at[k, c],
+                device_id={"rows": lax.rem(me_row + d + n_rows, n_rows)},
+                device_id_type=MESH,
+            )
+            there = jnp.logical_and(has_row(d), needed)
+            pl.when(there)(copy.start)
+            z_copies.append((copy, there))
+
+    forward(me_chan)
+    for copy, k in sorted(zip(y_copies, far), key=lambda pair: -far.index(pair[1])):
         copy.wait_recv()
-    groups = []
-    for k in range(c_mid // 8):
-        groups.append(jnp.concatenate([y_in[c][:, width * k : width * (k + 1)] for c in range(n_chan)], axis=1))
-    own = jnp.concatenate([*groups, jnp.zeros((32 - c_mid, n_chan * width), F32)], axis=0)
-    z_out[...] = own.astype(BF16)
-    z_copies = to_neighbours(z_out, z_in, zs_sem, zr_sem)
+        forward(chan_peers[k - 1])
+
+    def block(rows):
+        groups = [
+            jnp.concatenate([r[:, width * k : width * (k + 1)] for r in rows], axis=1) for k in range(c_mid // 8)
+        ]
+        return jnp.concatenate([*groups, jnp.zeros((32 - c_mid, n_chan * width), F32)], axis=0)
+
+    own = block([y_in[c] for c in range(n_chan)])
     pl.semaphore_wait(token_sem.at[0], rows_off(1))
     tell_rows(token_sem.at[1], 2)
-    from_neighbours(z_copies)
+    for k, (d, needed) in enumerate(((1, range(n_chan - halo, n_chan)), (-1, range(halo)))):
+
+        @pl.when(has_row(-d))
+        def _():
+            for c in needed:
+                pltpu.make_async_remote_copy(
+                    src_ref=y_in.at[c],
+                    dst_ref=z_in.at[k, c],
+                    send_sem=zs_sem.at[k, c],
+                    recv_sem=zr_sem.at[k, c],
+                    device_id={"rows": lax.rem(me_row + d + n_rows, n_rows)},
+                    device_id_type=MESH,
+                ).wait_recv()
+
     zero = jnp.zeros_like(own)
+    blank = jnp.zeros((8, 128), F32)
     state = jnp.concatenate(
         [
-            jnp.where(has_row(-1), z_in[0].astype(F32), zero),
+            jnp.where(has_row(-1), block([blank] * (n_chan - halo) + [z_in[0, c] for c in range(n_chan - halo, n_chan)]), zero),
             own,
-            jnp.where(has_row(1), z_in[1].astype(F32), zero),
+            jnp.where(has_row(1), block([z_in[1, c] for c in range(halo)] + [blank] * (n_chan - halo)), zero),
         ],
         axis=1,
     )
@@ -473,12 +509,13 @@
         back_out[c] = jnp.concatenate([piece[:8], piece[8:], jnp.zeros((8, 128 - 2 * width), F32)], axis=1)
     back_in[me_chan] = back_out[me_chan]
     back_copies = []
-    for k, peer in enumerate(chan_peers):
+    for k in far:
+        peer = chan_peers[k - 1]
         copy = pltpu.make_async_remote_copy(
             src_ref=back_out.at[peer],
             dst_ref=back_in.at[me_chan],
-            send_sem=bs_sem.at[k],
-            recv_sem=br_sem.at[n_chan - 2 - k],
+            send_sem=bs_sem.at[k - 1],
+            recv_sem=br_sem.at[k - 1],
             device_id={"chan": peer},
             device_id_type=MESH,
         )
@@ -546,12 +583,13 @@
     ll_out[...] = jnp.sum(partial, axis=0, keepdims=True)
     pl.semaphore_wait(token_sem.at[2], rows_off(4))
     ll_copies = []
-    for k, peer in enumerate(row_peers):
+    for k in far_rows:
+        peer = row_peers[k - 1]
         copy = pltpu.make_async_remote_copy(
             src_ref=ll_out,
-            dst_ref=ll_in.at[n_rows - 2 - k],
-            send_sem=ls_sem.at[k],
-            recv_sem=lr_sem.at[n_rows - 2 - k],
+            dst_ref=ll_in.at[n_rows - 1 - k],
+            send_sem=ls_sem.at[k - 1],
+            recv_sem=lr_sem.at[n_rows - 1 - k],
             device_id={"rows": peer},
             device_id_type=MESH,
         )
@@ -581,9 +619,10 @@
     loglik[...] = jnp.broadcast_to((jnp.sum(total) + const) * scale - 0.5 * log_two_pi, (1, 128))
     for copy in (*y_copies, *back_copies, *ll_copies):
         copy.wait_send()
-    for copies in (z_copies, k_copies):
-        for copy, d in copies:
-            pl.when(has_row(d))(copy.wait_send)
+    for copy, there in z_copies:
+        pl.when(there)(copy.wait_send)
+    for copy, d in k_copies:
+        pl.when(has_row(d))(copy.wait_send)
 
 
 def write_out(*refs):
@@ -668,8 +707,7 @@
             vmem((steps_p, c_top, 1), F32),
             vmem((n_chan, 8, 128), F32),
             vmem((n_chan, 8, 128), F32),
-            vmem((32, n_chan * width), BF16),
-            vmem((2, 32, n_chan * width), BF16),
+            vmem((2, n_chan, 8, 128), F32),
             vmem((16, n_chan * width), BF16),
             vmem((2, 16, n_chan * width), BF16),
             vmem((n_chan, 8, 128), F32),
@@ -682,8 +720,8 @@
             dma((len(small_args),)),
             dma((n_chan - 1,)),
             dma((n_chan - 1,)),
-            dma((2,)),
-            dma((2,)),
+            dma((2, n_chan)),
+            dma((2, n_chan)),
             dma((2,)),
             dma((2,)),
             dma((n_chan - 1,)),

time: 36.2 us -> 36.2 us (level)
  no operation moved by 1% of the time
where the time goes in v5:
time: 36.2 us; the launch traced here: 36.1 us
  Pallas kernels  35.5 us (98%)
  between operations  0.65 us (2%)
    pallas_call x1, Pallas kernels, body(): pl.pallas_call(functools.partial(kernel, n_rows, n_chan), out_shape=(vmem...  34.8 us

profile of v5, /device:TPU:6, one launch (start us, length us, event | category | flops | bytes accessed | tf_op | source)
XLA Modules:
  0.0 36.1 jit_solution(5884582465625671850)
XLA Ops:
  0.6 34.8 %shard_map.238 = (f32[96,32]{1,0:T(8,128)S(1)}, f32[64,48]{1,0:T(8,128)S(1)}, f32[1,128]{1,0:T(1,128)S(1)}) custom-call(f32[8,24,32]{2,1,0:T(8,128)} %bitcast.17, f32[3,24]{1,0:T(4,128)} %shift_mid_h.1, f32[3,24]{1,0:T(4,128)} %gain_mid_h.1, f32[3,24,24]{2,1,0:T(8,128)} %lower_mid_h.1, f32[3,24,24]{2,1,0:T(8,128)} %upper_mid_h.1, f32[3,24]{1,0:T(4,128)} %diag_mid_h.1, ...), custom_call_target="tpu_custom_call" | custom-call | tf_op jit(solution)/shard_map/pallas_call | solution.py:678
  35.5 0.7 %shard_map.239 = (f32[96,32]{1,0:T(8,128)}, f32[64,48]{1,0:T(8,128)}, f32[1,128]{1,0:T(1,128)}) custom-call(f32[96,32]{1,0:T(8,128)S(1)} %get-tuple-element.9.refs_0_, f32[64,48]{1,0:T(8,128)S(1)} %get-tuple-element.10.refs_1_, f32[1,128]{1,0:T(1,128)S(1)} %get-tuple-element.11.refs_2_), custom_call_target="tpu_custom_call" | custom-call | tf_op jit(solution)/shard_map/pallas_call | solution.py:761

commit v6 on v5

--- a/solution.py
+++ b/solution.py
@@ -172,6 +172,7 @@
     const_m,
     const_p,
     y_out,
+    y_half,
     y_in,
     z_in,
     k_out,
@@ -260,7 +261,14 @@
     far_rows = sorted(range(1, n_rows), key=lambda k: -min(k, n_rows - k))
     for k in far:
         pl.semaphore_signal(barrier, inc=1, device_id={"chan": chan_peers[k - 1]}, device_id_type=MESH)
-    tell_rows(barrier, 1)
+    for d in (1, -1):
+
+        @pl.when(has_row(d))
+        def _():
+            row = lax.rem(me_row + d + n_rows, n_rows)
+            for k in (*far, 0):
+                pl.semaphore_signal(barrier, inc=1, device_id={"rows": row, "chan": me_chan ^ k}, device_id_type=MESH)
+
 
     loads = [
         pltpu.make_async_copy(src, dst, load_sem.at[k])
@@ -307,23 +315,49 @@
         packed = [row[8 * k : 8 * k + 8] for k in range(c_mid // 8)]
         packed.append(jnp.zeros((8, 128 - width * (c_mid // 8)), F32))
         y_out[i] = jnp.concatenate(packed, axis=1)
+        y_half[i] = y_out[i].astype(BF16)
     y_in[me_chan] = y_out[me_chan]
 
-    pl.semaphore_wait(barrier, n_chan - 1 + rows_off(1))
+    pl.semaphore_wait(barrier, n_chan - 1 + n_chan * rows_off(1))
     tell_rows(token_sem.at[0], 1)
-    y_copies = []
-    for k in far:
-        peer = chan_peers[k - 1]
-        copy = pltpu.make_async_remote_copy(
-            src_ref=y_out.at[peer],
+    y_copies = {
+        c: pltpu.make_async_remote_copy(
+            src_ref=y_out.at[me_chan ^ c],
             dst_ref=y_in.at[me_chan],
-            send_sem=ys_sem.at[k - 1],
-            recv_sem=yr_sem.at[k - 1],
-            device_id={"chan": peer},
+            send_sem=ys_sem.at[c - 1],
+            recv_sem=yr_sem.at[c - 1],
+            device_id={"chan": me_chan ^ c},
             device_id_type=MESH,
         )
-        copy.start()
-        y_copies.append(copy)
+        for c in far
+    }
+    z_copies = []
+    for k, (d, needed) in enumerate(((1, me_chan >= n_chan - halo), (-1, me_chan < halo))):
+        copies = {
+            c: pltpu.make_async_remote_copy(
+                src_ref=y_half.at[me_chan ^ c],
+                dst_ref=z_in.at[k, me_chan],
+                send_sem=zs_sem.at[k, c],
+                recv_sem=zr_sem.at[k, me_chan],
+                device_id={"rows": lax.rem(me_row + d + n_rows, n_rows), "chan": me_chan ^ c},
+                device_id_type=MESH,
+            )
+            for c in (*far, 0)
+        }
+        z_copies.append((copies, jnp.logical_and(has_row(d), needed)))
+    for group in (far[:2], far[2:] + [0]):
+        for c in group:
+            if c:
+                y_copies[c].start()
+        for copies, there in z_copies:
+
+            @pl.when(there)
+            def _():
+                for c in group:
+                    copies[c].start()
+
+    y_copies = list(y_copies.values())
+    z_copies = [(list(copies.values()), there) for copies, there in z_copies]
 
     for load in smalls:
         load.wait()
@@ -398,26 +432,8 @@
     bias3_m = [column(third_bias_mid[s : s + 1]) for s in range(steps_m)]
     bias3_p = [column(third_bias_top[s : s + 1]) for s in range(steps_p)]
 
-    z_copies = []
-
-    def forward(c):
-        for k, (d, needed) in enumerate(((1, c >= n_chan - halo), (-1, c < halo))):
-            copy = pltpu.make_async_remote_copy(
-                src_ref=y_in.at[c],
-                dst_ref=z_in.at[k, c],
-                send_sem=zs_sem.at[k, c],
-                recv_sem=zr_sem.at[k, c],
-                device_id={"rows": lax.rem(me_row + d + n_rows, n_rows)},
-                device_id_type=MESH,
-            )
-            there = jnp.logical_and(has_row(d), needed)
-            pl.when(there)(copy.start)
-            z_copies.append((copy, there))
-
-    forward(me_chan)
-    for copy, k in sorted(zip(y_copies, far), key=lambda pair: -far.index(pair[1])):
+    for copy in y_copies:
         copy.wait_recv()
-        forward(chan_peers[k - 1])
 
     def block(rows):
         groups = [
@@ -434,7 +450,7 @@
         def _():
             for c in needed:
                 pltpu.make_async_remote_copy(
-                    src_ref=y_in.at[c],
+                    src_ref=y_half.at[c],
                     dst_ref=z_in.at[k, c],
                     send_sem=zs_sem.at[k, c],
                     recv_sem=zr_sem.at[k, c],
@@ -446,9 +462,9 @@
     blank = jnp.zeros((8, 128), F32)
     state = jnp.concatenate(
         [
-            jnp.where(has_row(-1), block([blank] * (n_chan - halo) + [z_in[0, c] for c in range(n_chan - halo, n_chan)]), zero),
+            jnp.where(has_row(-1), block([blank] * (n_chan - halo) + [z_in[0, c].astype(F32) for c in range(n_chan - halo, n_chan)]), zero),
             own,
-            jnp.where(has_row(1), block([z_in[1, c] for c in range(halo)] + [blank] * (n_chan - halo)), zero),
+            jnp.where(has_row(1), block([z_in[1, c].astype(F32) for c in range(halo)] + [blank] * (n_chan - halo)), zero),
         ],
         axis=1,
     )
@@ -619,8 +635,13 @@
     loglik[...] = jnp.broadcast_to((jnp.sum(total) + const) * scale - 0.5 * log_two_pi, (1, 128))
     for copy in (*y_copies, *back_copies, *ll_copies):
         copy.wait_send()
-    for copy, there in z_copies:
-        pl.when(there)(copy.wait_send)
+    for copies, there in z_copies:
+
+        @pl.when(there)
+        def _():
+            for copy in copies:
+                copy.wait_send()
+
     for copy, d in k_copies:
         pl.when(has_row(d))(copy.wait_send)
 
@@ -706,8 +727,9 @@
             vmem((steps_m, 32, 1), F32),
             vmem((steps_p, c_top, 1), F32),
             vmem((n_chan, 8, 128), F32),
+            vmem((n_chan, 8, 128), BF16),
             vmem((n_chan, 8, 128), F32),
-            vmem((2, n_chan, 8, 128), F32),
+            vmem((2, n_chan, 8, 128), BF16),
             vmem((16, n_chan * width), BF16),
             vmem((2, 16, n_chan * width), BF16),
             vmem((n_chan, 8, 128), F32),

time: 36.2 us -> 34.8 us (0.961)
  Pallas kernels: 35.5 us -> 34 us
    pallas_call x1, Pallas kernels: 34.8 us -> 33.4 us  [body(): pl.pallas_call(functools.partial(kernel, n_rows, n_chan), out_shape=(vmem...]
where the time goes in v6:
time: 34.8 us; the launch traced here: 34.7 us
  Pallas kernels  34 us (98%)
  between operations  0.65 us (2%)
    pallas_call x1, Pallas kernels, body(): pl.pallas_call(functools.partial(kernel, n_rows, n_chan), out_shape=(vmem...  33.4 us

profile of v6, /device:TPU:6, one launch (start us, length us, event | category | flops | bytes accessed | tf_op | source)
XLA Modules:
  0.0 34.7 jit_solution(12885152415762582122)
XLA Ops:
  0.6 33.4 %shard_map.238 = (f32[96,32]{1,0:T(8,128)S(1)}, f32[64,48]{1,0:T(8,128)S(1)}, f32[1,128]{1,0:T(1,128)S(1)}) custom-call(f32[8,24,32]{2,1,0:T(8,128)} %bitcast.17, f32[3,24]{1,0:T(4,128)} %shift_mid_h.1, f32[3,24]{1,0:T(4,128)} %gain_mid_h.1, f32[3,24,24]{2,1,0:T(8,128)} %lower_mid_h.1, f32[3,24,24]{2,1,0:T(8,128)} %upper_mid_h.1, f32[3,24]{1,0:T(4,128)} %diag_mid_h.1, ...), custom_call_target="tpu_custom_call" | custom-call | tf_op jit(solution)/shard_map/pallas_call | solution.py:699
  34.0 0.7 %shard_map.239 = (f32[96,32]{1,0:T(8,128)}, f32[64,48]{1,0:T(8,128)}, f32[1,128]{1,0:T(1,128)}) custom-call(f32[96,32]{1,0:T(8,128)S(1)} %get-tuple-element.9.refs_0_, f32[64,48]{1,0:T(8,128)S(1)} %get-tuple-element.10.refs_1_, f32[1,128]{1,0:T(1,128)S(1)} %get-tuple-element.11.refs_2_), custom_call_target="tpu_custom_call" | custom-call | tf_op jit(solution)/shard_map/pallas_call | solution.py:783

commit v7 on v6

--- a/solution.py
+++ b/solution.py
@@ -119,7 +119,7 @@
 
 
 def log_sigmoid(g):
-    return jnp.minimum(g, 0.0) - jnp.log1p(jnp.exp(-jnp.abs(g)))
+    return jnp.minimum(g, 0.0) - jnp.log(1.0 + jnp.exp(-jnp.abs(g)))
 
 
 def kernel(
@@ -257,18 +257,26 @@
     barrier = pltpu.get_barrier_semaphore()
     far = sorted(range(1, n_chan), key=lambda k: (-(k // 2 == 2), -(k > 1)))
     chan_peers = [me_chan ^ k for k in range(1, n_chan)]
-    row_peers = [lax.rem(me_row + k, n_rows) for k in range(1, n_rows)]
-    far_rows = sorted(range(1, n_rows), key=lambda k: -min(k, n_rows - k))
-    for k in far:
-        pl.semaphore_signal(barrier, inc=1, device_id={"chan": chan_peers[k - 1]}, device_id_type=MESH)
-    for d in (1, -1):
-
+
+    def tell_block(d, group):
         @pl.when(has_row(d))
         def _():
-            row = lax.rem(me_row + d + n_rows, n_rows)
-            for k in (*far, 0):
-                pl.semaphore_signal(barrier, inc=1, device_id={"rows": row, "chan": me_chan ^ k}, device_id_type=MESH)
-
+            for k in group:
+                pl.semaphore_signal(
+                    barrier, inc=1, device_id={"rows": me_row + d, "chan": me_chan ^ k}, device_id_type=MESH
+                )
+
+    def tell_chan(group):
+        for k in group:
+            pl.semaphore_signal(barrier, inc=1, device_id={"chan": me_chan ^ k}, device_id_type=MESH)
+
+    near = [0, *(k for k in range(1, n_chan) if k // 2 == 0)]
+    rest = [k for k in far if k not in near]
+    tell_block(-1, near)
+    tell_block(1, near)
+    tell_chan(far)
+    tell_block(-1, rest)
+    tell_block(1, rest)
 
     loads = [
         pltpu.make_async_copy(src, dst, load_sem.at[k])
@@ -318,6 +326,31 @@
         y_half[i] = y_out[i].astype(BF16)
     y_in[me_chan] = y_out[me_chan]
 
+    for load in smalls:
+        load.wait()
+    src, lane = iota2((c_top, 192), 0), lax.rem(iota2((c_top, 192), 1), 64)
+    squeezed_place = jnp.where(
+        jnp.logical_and(lax.rem(lane, 16) < half_m, src == 4 * lax.rem(lane, 16) + lax.div(lane, 16)), 1.0, 0.0
+    )
+    src, lane = iota2((c_top, 144), 0), lax.rem(iota2((c_top, 144), 1), 48)
+    top_place = jnp.where(src == lane, 1.0, 0.0)
+    for s in range(steps_p):
+        mix, const = mixing(
+            lower_top[s],
+            upper_top[s],
+            diag_top[s : s + 1],
+            gain_top[s : s + 1],
+            shift_top[s : s + 1],
+            None,
+            squeezed_place if s == 0 else top_place,
+            128 if s == 0 else 96,
+        )
+        if s == 0:
+            mix_p0[...] = mix
+        else:
+            mix_p1[s - 1] = mix
+        const_p[s] = const
+
     pl.semaphore_wait(barrier, n_chan - 1 + n_chan * rows_off(1))
     tell_rows(token_sem.at[0], 1)
     y_copies = {
@@ -359,8 +392,6 @@
     y_copies = list(y_copies.values())
     z_copies = [(list(copies.values()), there) for copies, there in z_copies]
 
-    for load in smalls:
-        load.wait()
     spread = jnp.where(
         iota2((32, c_mid), 0)
         == iota2((32, c_mid), 1) + jnp.where(iota2((32, c_mid), 1) >= half_m, 16 - half_m, 0),
@@ -383,28 +414,6 @@
         )
         mix_m[s] = mix
         const_m[s] = jnp.where(iota2((32, 1), 0) == half_m, 1.0, const)
-    src, lane = iota2((c_top, 192), 0), lax.rem(iota2((c_top, 192), 1), 64)
-    squeezed_place = jnp.where(
-        jnp.logical_and(lax.rem(lane, 16) < half_m, src == 4 * lax.rem(lane, 16) + lax.div(lane, 16)), 1.0, 0.0
-    )
-    src, lane = iota2((c_top, 144), 0), lax.rem(iota2((c_top, 144), 1), 48)
-    top_place = jnp.where(src == lane, 1.0, 0.0)
-    for s in range(steps_p):
-        mix, const = mixing(
-            lower_top[s],
-            upper_top[s],
-            diag_top[s : s + 1],
-            gain_top[s : s + 1],
-            shift_top[s : s + 1],
-            None,
-            squeezed_place if s == 0 else top_place,
-            128 if s == 0 else 96,
-        )
-        if s == 0:
-            mix_p0[...] = mix
-        else:
-            mix_p1[s - 1] = mix
-        const_p[s] = const
 
     def prepare_mid(s):
         w1f_m[...] = jnp.zeros_like(w1f_m)
@@ -513,10 +522,12 @@
         )
         state = jnp.concatenate([ua, updated], axis=0)
         mine = g[:, own_at : own_at + own_lanes]
-        partial = partial + folded(jnp.where(valid_m, log_sigmoid(mine), 0.0))
+        if s < steps_m - 1:
+            partial = partial + folded(jnp.where(valid_m, log_sigmoid(mine), 0.0))
     kept = state[16:, own_at : own_at + own_lanes]
     k_out[...] = kept.astype(BF16)
     k_copies = to_neighbours(k_out, k_in, ks_sem, kr_sem)
+    partial = partial + folded(jnp.where(valid_m, log_sigmoid(mine), 0.0))
     latent = jnp.where(valid_m, state[:16, own_at : own_at + own_lanes], 0.0)
     partial = partial + folded(-0.5 * latent * latent)
 
@@ -598,6 +609,8 @@
     partial = partial + folded(jnp.where(mine_p, -0.5 * state * state, 0.0))
     ll_out[...] = jnp.sum(partial, axis=0, keepdims=True)
     pl.semaphore_wait(token_sem.at[2], rows_off(4))
+    row_peers = [lax.rem(me_row + k, n_rows) for k in range(1, n_rows)]
+    far_rows = sorted(range(1, n_rows), key=lambda k: -min(k, n_rows - k))
     ll_copies = []
     for k in far_rows:
         peer = row_peers[k - 1]

time: 34.8 us -> 35.4 us (1.017)
  Pallas kernels: 34 us -> 34.6 us
    pallas_call x1, Pallas kernels: 33.4 us -> 34 us  [body(): pl.pallas_call(functools.partial(kernel, n_rows, n_chan), out_shape=(vmem...]
where the time goes in v7:
time: 35.4 us; the launch traced here: 35.3 us
  Pallas kernels  34.6 us (98%)
  between operations  0.65 us (2%)
    pallas_call x1, Pallas kernels, body(): pl.pallas_call(functools.partial(kernel, n_rows, n_chan), out_shape=(vmem...  34 us

profile of v7, /device:TPU:6, one launch (start us, length us, event | category | flops | bytes accessed | tf_op | source)
XLA Modules:
  0.0 35.3 jit_solution(14010514347400465506)
XLA Ops:
  0.6 34.0 %shard_map.238 = (f32[96,32]{1,0:T(8,128)S(1)}, f32[64,48]{1,0:T(8,128)S(1)}, f32[1,128]{1,0:T(1,128)S(1)}) custom-call(f32[8,24,32]{2,1,0:T(8,128)} %bitcast.17, f32[3,24]{1,0:T(4,128)} %shift_mid_h.1, f32[3,24]{1,0:T(4,128)} %gain_mid_h.1, f32[3,24,24]{2,1,0:T(8,128)} %lower_mid_h.1, f32[3,24,24]{2,1,0:T(8,128)} %upper_mid_h.1, f32[3,24]{1,0:T(4,128)} %diag_mid_h.1, ...), custom_call_target="tpu_custom_call" | custom-call | tf_op jit(solution)/shard_map/pallas_call | solution.py:712
  34.6 0.7 %shard_map.239 = (f32[96,32]{1,0:T(8,128)}, f32[64,48]{1,0:T(8,128)}, f32[1,128]{1,0:T(1,128)}) custom-call(f32[96,32]{1,0:T(8,128)S(1)} %get-tuple-element.9.refs_0_, f32[64,48]{1,0:T(8,128)S(1)} %get-tuple-element.10.refs_1_, f32[1,128]{1,0:T(1,128)S(1)} %get-tuple-element.11.refs_2_), custom_call_target="tpu_custom_call" | custom-call | tf_op jit(solution)/shard_map/pallas_call | solution.py:796

commit v8 on v6

--- a/solution.py
+++ b/solution.py
@@ -119,7 +119,7 @@
 
 
 def log_sigmoid(g):
-    return jnp.minimum(g, 0.0) - jnp.log1p(jnp.exp(-jnp.abs(g)))
+    return jnp.minimum(g, 0.0) - jnp.log(1.0 + jnp.exp(-jnp.abs(g)))
 
 
 def kernel(
@@ -257,18 +257,26 @@
     barrier = pltpu.get_barrier_semaphore()
     far = sorted(range(1, n_chan), key=lambda k: (-(k // 2 == 2), -(k > 1)))
     chan_peers = [me_chan ^ k for k in range(1, n_chan)]
-    row_peers = [lax.rem(me_row + k, n_rows) for k in range(1, n_rows)]
-    far_rows = sorted(range(1, n_rows), key=lambda k: -min(k, n_rows - k))
-    for k in far:
-        pl.semaphore_signal(barrier, inc=1, device_id={"chan": chan_peers[k - 1]}, device_id_type=MESH)
-    for d in (1, -1):
-
+
+    def tell_block(d, group):
         @pl.when(has_row(d))
         def _():
-            row = lax.rem(me_row + d + n_rows, n_rows)
-            for k in (*far, 0):
-                pl.semaphore_signal(barrier, inc=1, device_id={"rows": row, "chan": me_chan ^ k}, device_id_type=MESH)
-
+            for k in group:
+                pl.semaphore_signal(
+                    barrier, inc=1, device_id={"rows": me_row + d, "chan": me_chan ^ k}, device_id_type=MESH
+                )
+
+    def tell_chan(group):
+        for k in group:
+            pl.semaphore_signal(barrier, inc=1, device_id={"chan": me_chan ^ k}, device_id_type=MESH)
+
+    near = [0, *(k for k in range(1, n_chan) if k // 2 == 0)]
+    rest = [k for k in far if k not in near]
+    tell_block(-1, near)
+    tell_block(1, near)
+    tell_chan(far)
+    tell_block(-1, rest)
+    tell_block(1, rest)
 
     loads = [
         pltpu.make_async_copy(src, dst, load_sem.at[k])
@@ -383,6 +391,7 @@
         )
         mix_m[s] = mix
         const_m[s] = jnp.where(iota2((32, 1), 0) == half_m, 1.0, const)
+
     src, lane = iota2((c_top, 192), 0), lax.rem(iota2((c_top, 192), 1), 64)
     squeezed_place = jnp.where(
         jnp.logical_and(lax.rem(lane, 16) < half_m, src == 4 * lax.rem(lane, 16) + lax.div(lane, 16)), 1.0, 0.0
@@ -513,10 +522,12 @@
         )
         state = jnp.concatenate([ua, updated], axis=0)
         mine = g[:, own_at : own_at + own_lanes]
-        partial = partial + folded(jnp.where(valid_m, log_sigmoid(mine), 0.0))
+        if s < steps_m - 1:
+            partial = partial + folded(jnp.where(valid_m, log_sigmoid(mine), 0.0))
     kept = state[16:, own_at : own_at + own_lanes]
     k_out[...] = kept.astype(BF16)
     k_copies = to_neighbours(k_out, k_in, ks_sem, kr_sem)
+    partial = partial + folded(jnp.where(valid_m, log_sigmoid(mine), 0.0))
     latent = jnp.where(valid_m, state[:16, own_at : own_at + own_lanes], 0.0)
     partial = partial + folded(-0.5 * latent * latent)
 
@@ -598,6 +609,8 @@
     partial = partial + folded(jnp.where(mine_p, -0.5 * state * state, 0.0))
     ll_out[...] = jnp.sum(partial, axis=0, keepdims=True)
     pl.semaphore_wait(token_sem.at[2], rows_off(4))
+    row_peers = [lax.rem(me_row + k, n_rows) for k in range(1, n_rows)]
+    far_rows = sorted(range(1, n_rows), key=lambda k: -min(k, n_rows - k))
     ll_copies = []
     for k in far_rows:
         peer = row_peers[k - 1]
@@ -626,6 +639,17 @@
             (cells // 4) * (jnp.sum(gain_top[...]) + jnp.sum(diag_top[...])),
         )
     )
+    for copy in (*y_copies, *back_copies, *ll_copies):
+        copy.wait_send()
+    for copies, there in z_copies:
+
+        @pl.when(there)
+        def _():
+            for copy in copies:
+                copy.wait_send()
+
+    for copy, d in k_copies:
+        pl.when(has_row(d))(copy.wait_send)
     for copy in ll_copies:
         copy.wait_recv()
     total = ll_out[...]
@@ -633,17 +657,6 @@
         total = total + ll_in[k]
     scale = 1.0 / (c_mid * cells)
     loglik[...] = jnp.broadcast_to((jnp.sum(total) + const) * scale - 0.5 * log_two_pi, (1, 128))
-    for copy in (*y_copies, *back_copies, *ll_copies):
-        copy.wait_send()
-    for copies, there in z_copies:
-
-        @pl.when(there)
-        def _():
-            for copy in copies:
-                copy.wait_send()
-
-    for copy, d in k_copies:
-        pl.when(has_row(d))(copy.wait_send)
 
 
 def write_out(*refs):

time: 34.8 us -> 34.7 us (level)
  no operation moved by 1% of the time
where the time goes in v8:
time: 34.7 us; the launch traced here: 34.6 us
  Pallas kernels  34 us (98%)
  between operations  0.65 us (2%)
    pallas_call x1, Pallas kernels, body(): pl.pallas_call(functools.partial(kernel, n_rows, n_chan), out_shape=(vmem...  33.3 us

profile of v8, /device:TPU:6, one launch (start us, length us, event | category | flops | bytes accessed | tf_op | source)
XLA Modules:
  0.0 34.6 jit_solution(2373591129983775127)
XLA Ops:
  0.6 33.3 %shard_map.238 = (f32[96,32]{1,0:T(8,128)S(1)}, f32[64,48]{1,0:T(8,128)S(1)}, f32[1,128]{1,0:T(1,128)S(1)}) custom-call(f32[8,24,32]{2,1,0:T(8,128)} %bitcast.17, f32[3,24]{1,0:T(4,128)} %shift_mid_h.1, f32[3,24]{1,0:T(4,128)} %gain_mid_h.1, f32[3,24,24]{2,1,0:T(8,128)} %lower_mid_h.1, f32[3,24,24]{2,1,0:T(8,128)} %upper_mid_h.1, f32[3,24]{1,0:T(4,128)} %diag_mid_h.1, ...), custom_call_target="tpu_custom_call" | custom-call | tf_op jit(solution)/shard_map/pallas_call | solution.py:712
  34.0 0.7 %shard_map.239 = (f32[96,32]{1,0:T(8,128)}, f32[64,48]{1,0:T(8,128)}, f32[1,128]{1,0:T(1,128)}) custom-call(f32[96,32]{1,0:T(8,128)S(1)} %get-tuple-element.9.refs_0_, f32[64,48]{1,0:T(8,128)S(1)} %get-tuple-element.10.refs_1_, f32[1,128]{1,0:T(1,128)S(1)} %get-tuple-element.11.refs_2_), custom_call_target="tpu_custom_call" | custom-call | tf_op jit(solution)/shard_map/pallas_call | solution.py:796
